TPU v7x, 32 devices: a whole 2x2x4 slice. The times are simulated.
32 devices in a mesh: mem: 16 (over z, y, core), band: 2 (over x).
Axes of the slice: x: 2, y: 2, z: 4, core: 2. Of those that a mesh axis runs over, the one named last changes fastest.
Arguments:
- ensemble: bfloat16 [16, 12, 32, 128], P('mem', None, 'band'), may hold values from -6 to 6
- alpha: float32 [16, 12, 32, 128], P('mem', None, 'band'), may hold values from -6 to 6
- lat_lower: int32 [96], P('band'), may hold values from -1 to 15, as said below
- lat_weight: float32 [96], P('band'), may hold values from 0 to 1
- background: float32 [12, 32, 1152], P(None, ('band', 'mem')), may hold values from -6 to 6
- obs_cell: int32 [32, 256], P(('band', 'mem')), may hold values from 0 to 1151
- obs_value: float32 [12, 32, 256], P(None, ('band', 'mem')), may hold values from -6 to 6
- obs_precision: float32 [32, 256], P(('band', 'mem')), may hold values from 1 to 10
Outputs:
- advected: float32 [12, 32, 1152], P(None, ('band', 'mem'))
- gradient: float32 [16, 12, 32, 128], P('mem', None, 'band')
Inputs may be any that keep to these rules, and one draw needn't show every extreme that they name: `lat_lower`: fine rows of the first band use lower rows from 0, those of the last band up to 14 of their band, so that their upper row reaches 15; other bands reach -1 and 15. `obs_cell`: the cell is r * 24 + c for fine row r and column c within the tile.
All inputs are finite; a program needn't handle non-finite values.
Results may differ from a plain program's by a relative error of at most 0.0004.
Values sent between devices are 32-bit elements; how exact they have to be, the bound alone decides.
A program may use at most 64 MiB of HBM per device.

v0:
```python
import functools
import math

import jax
import jax.numpy as jnp
from jax import lax
from jax.experimental import pallas as pl
from jax.experimental.pallas import tpu as pltpu
from jax.sharding import PartitionSpec as P

advect_rate = 0.25
LANES = 128
f32 = jnp.float32
bf16 = jnp.bfloat16


def split2(x):
    hi = x.astype(bf16)
    lo = (x - hi.astype(f32)).astype(bf16)
    return hi, lo


def dims(a, b, ca, cb):
    return lax.dot_general(a, b, (((ca,), (cb,)), ((), ())), preferred_element_type=f32)


def smooth_lon(x):
    n = x.shape[1]
    return 0.25 * pltpu.roll(x, 1, 1) + 0.5 * x + 0.25 * pltpu.roll(x, n - 1, 1)


def kernel(
    cfg,
    ens_ref,
    alpha_ref,
    low_ref,
    wt_ref,
    bg_ref,
    cell_ref,
    val_ref,
    prec_ref,
    adv_ref,
    grad_ref,
    ensf,
    edge_send,
    edge_recv,
    partial_rows,
    send1,
    recv1,
    sum1,
    place,
    table_hi,
    table_lo,
    frame_rows,
    frame_recv,
    send2,
    recv2,
    merged,
    coarse,
    edge_ss,
    edge_rs,
    frame_ss,
    frame_rs,
    ss1,
    rs1,
    ss2,
    rs2,
    bg_recv,
    bg_ss,
    bg_rs,
):
    n, nb, lev, rows, lon, fine_rows, fine_cols, scale = cfg
    block = lon // n
    frame = block + 2
    ratio = fine_cols // block
    cells = fine_rows * fine_cols
    wrows = recv1.shape[1]
    per = LANES // frame
    order = list(range(1, rows - 1)) + [-1, 0, rows - 1, rows]
    slot = {k: i for i, k in enumerate(order)}
    up_at = (rows - 2) * lev
    down_at = rows * lev
    groups = partial_rows.shape[0] // LANES
    me = lax.axis_index("mem")
    band = lax.axis_index("band")
    has_up = band > 0
    has_down = band < nb - 1

    barrier = pltpu.get_barrier_semaphore()

    def greet(o, c):
        pl.semaphore_signal(barrier, inc=1, device_id={"mem": lax.rem(me + o, n)})
        return c

    lax.fori_loop(1, n, greet, 0)

    @pl.when(has_up)
    def _():
        pl.semaphore_signal(barrier, inc=1, device_id={"band": band - 1})

    @pl.when(has_down)
    def _():
        pl.semaphore_signal(barrier, inc=1, device_id={"band": band + 1})

    ensf[...] = ens_ref[...].astype(f32)

    def row(ref, k):
        parts = [ref.at[t][pl.ds(k, lev, stride=rows), :] for t in range(lon // LANES)]
        return parts[0] if len(parts) == 1 else jnp.concatenate(parts, axis=1)

    for side, ks in ((0, (0, 1)), (1, (rows - 1, rows - 2))):
        edge_send[side, 0, 0:lev, :] = row(alpha_ref, ks[0])
        edge_send[side, 1, 0:lev, :] = row(alpha_ref, ks[1])
        edge_send[side, 2, 0:lev, :] = row(ensf, ks[0])

    if nb == 2:
        pl.semaphore_wait(barrier, n)
    else:
        pl.semaphore_wait(barrier, n - 1 + has_up.astype(jnp.int32) + has_down.astype(jnp.int32))

    def edge_copy(side):
        return pltpu.make_async_remote_copy(
            src_ref=edge_send.at[side],
            dst_ref=edge_recv.at[1 - side],
            send_sem=edge_ss.at[side],
            recv_sem=edge_rs.at[1 - side],
            device_id={"band": band - 1 if side == 0 else band + 1},
        )

    def frame_copy(side):
        at = up_at if side == 0 else down_at
        return pltpu.make_async_remote_copy(
            src_ref=frame_rows.at[pl.ds(at, 2 * lev), :],
            dst_ref=frame_recv.at[1 - side],
            send_sem=frame_ss.at[side],
            recv_sem=frame_rs.at[1 - side],
            device_id={"band": band - 1 if side == 0 else band + 1},
        )

    def start_band(copy, recv):
        for side, has in ((0, has_up), (1, has_down)):

            @pl.when(has)
            def _():
                copy(side).start()

            @pl.when(jnp.logical_not(has))
            def _():
                recv[side] = jnp.zeros(recv.shape[1:], f32)

    def wait_band(copy):
        for side, has in ((0, has_up), (1, has_down)):

            @pl.when(has)
            def _():
                copy(side).wait_send()
                copy(1 - side).wait_recv()

    start_band(edge_copy, edge_recv)

    def bg_copy(side):
        return pltpu.make_async_remote_copy(
            src_ref=bg_ref,
            dst_ref=bg_recv.at[1 - side],
            send_sem=bg_ss.at[side],
            recv_sem=bg_rs.at[1 - side],
            device_id={"mem": lax.rem(me + (n - 1 if side == 0 else 1), n)},
        )

    bg_copy(0).start()
    bg_copy(1).start()

    fr = lax.broadcasted_iota(jnp.int32, (fine_rows, cells), 0)
    fc = lax.broadcasted_iota(jnp.int32, (fine_rows, cells), 1)
    pick = (fc // fine_cols == fr).astype(bf16)
    w_hi = wt_ref[...].astype(bf16)
    rest = wt_ref[...] - w_hi.astype(f32)
    w_mid = rest.astype(bf16)
    w_lo = (rest - w_mid.astype(f32)).astype(bf16)
    low_b = low_ref[...].astype(f32).astype(bf16)
    rowvec = jnp.concatenate([jnp.broadcast_to(v, (8, fine_rows)) for v in (w_hi.astype(f32), w_mid.astype(f32), w_lo.astype(f32), low_b.astype(f32))], axis=0)
    spread = dims(rowvec.astype(bf16), pick, 1, 0)
    wcell = spread[0:1] + spread[8:9] + spread[16:17]
    lcell = spread[24:25].astype(jnp.int32)
    cell = lax.broadcasted_iota(jnp.int32, (1, cells), 1)
    col = cell % fine_cols

    def lon_parts(shift):
        num = 2 * (col + shift) + 1 + ratio
        return num // (2 * ratio), (num % (2 * ratio)).astype(f32) / (2 * ratio)

    q0, f0 = lon_parts(0)
    qn, fn = lon_parts(1)
    qp, fp = lon_parts(-1)
    chunk = 32

    def table_step(i, c):
        kap = lax.broadcasted_iota(jnp.int32, (chunk, 1), 0) + i * chunk
        lane = kap % LANES
        k = (kap // LANES) * per + lane // frame
        w = lane % frame
        ok = lane < per * frame
        k = jnp.where(ok, k, -5)
        w = jnp.where(ok, w, -5)
        latv = jnp.where(k == lcell + 1, 1.0 - wcell, 0.0) + jnp.where(k == lcell + 2, wcell, 0.0)

        def lonv(q, f):
            return jnp.where(w == q, 1.0 - f, 0.0) + jnp.where(w == q + 1, f, 0.0)

        at = pl.ds(pl.multiple_of(i * chunk, chunk), chunk)
        hi, lo = split2(latv * lonv(q0, f0))
        table_hi[at, 0:cells] = hi
        table_lo[at, 0:cells] = lo
        hi, lo = split2(latv * (0.5 * (lonv(qn, fn) - lonv(qp, fp))))
        table_hi[at, cells : 2 * cells] = hi
        table_lo[at, cells : 2 * cells] = lo
        return c

    lax.fori_loop(0, table_hi.shape[0] // chunk, table_step, 0)

    nobs = cell_ref.shape[1]
    prec = prec_ref[...]
    lhs = jnp.concatenate([prec * val_ref[:, 0, :], prec, jnp.zeros((16 - lev - 1, nobs), f32)], axis=0)
    l_hi = lhs.astype(bf16).astype(f32)
    l_mid = (lhs - l_hi).astype(bf16).astype(f32)
    l_lo = lhs - l_hi - l_mid
    l3 = jnp.concatenate([l_hi, l_mid, l_lo], axis=0).astype(bf16)
    hot = (lax.broadcasted_iota(jnp.int32, (cells, nobs), 0) == cell_ref[...]).astype(f32).astype(bf16)
    obs = dims(l3, hot, 1, 1)
    obs = obs[0:16] + obs[16:32] + obs[32:48]
    obs_b = obs[0:lev]
    obs_a = obs[lev : lev + 1]
    partial_rows[...] = jnp.zeros(partial_rows.shape, f32)
    frame_rows[...] = jnp.zeros(frame_rows.shape, f32)
    send1[...] = jnp.zeros(send1.shape, f32)
    send2[...] = jnp.zeros(send2.shape, f32)
    back = bg_ref[:, 0, :]
    for side in (0, 1):
        bg_copy(side).wait()
    from_left, from_right = bg_recv[0, :, 0, :], bg_recv[1, :, 0, :]
    before = jnp.where(col == 0, pltpu.roll(from_left, cells - fine_cols + 1, 1), pltpu.roll(back, 1, 1))
    after = jnp.where(
        col == fine_cols - 1, pltpu.roll(from_right, fine_cols - 1, 1), pltpu.roll(back, cells - 1, 1)
    )
    back_slope = 0.5 * (after - before)

    wait_band(edge_copy)

    def alpha_row(k):
        if k < 0:
            return edge_recv[0, -1 - k, 0:lev, :]
        if k >= rows:
            return edge_recv[1, k - rows, 0:lev, :]
        return row(alpha_ref, k)

    def ens_row(k):
        if k < 0:
            return edge_recv[0, 2, 0:lev, :]
        if k >= rows:
            return edge_recv[1, 2, 0:lev, :]
        return row(ensf, k)

    for k in range(-1, rows + 1):
        s = 0.25 * alpha_row(k - 1) + 0.5 * alpha_row(k) + 0.25 * alpha_row(k + 1)
        partial_rows[slot[k] * lev : (slot[k] + 1) * lev, :] = smooth_lon(s) * ens_row(k) * scale

    for g in range(groups):
        for t in range(lon // LANES):
            piece = partial_rows[g * LANES : (g + 1) * LANES, t * LANES : (t + 1) * LANES].T
            send1[pl.ds(groups * (t * LANES + 1) + g, LANES, stride=groups), :] = piece
    send1[0:groups, :] = send1[groups * lon : groups * (lon + 1), :]
    send1[groups * (lon + 1) : groups * (lon + 2), :] = send1[groups : 2 * groups, :]

    step = groups * block

    def copy1(dst):
        return pltpu.make_async_remote_copy(
            src_ref=send1.at[pl.ds(pl.multiple_of(dst * step, step), wrows), :],
            dst_ref=recv1.at[me],
            send_sem=ss1.at[dst],
            recv_sem=rs1.at[me],
            device_id={"mem": dst},
        )

    def copy2(dst):
        return pltpu.make_async_remote_copy(
            src_ref=send2,
            dst_ref=recv2.at[me],
            send_sem=ss2.at[dst],
            recv_sem=rs2.at[me],
            device_id={"mem": dst},
        )

    def start_all(copy):
        def go(o, c):
            copy(lax.rem(me + o, n)).start()
            return c

        lax.fori_loop(1, n, go, 0)

    def wait_all(copy, recv, ss, rs):
        def go(o, c):
            src = lax.rem(me + o, n)
            pltpu.make_async_copy(recv.at[src], recv.at[src], rs.at[src]).wait()
            copy(src).wait_send()
            return c

        lax.fori_loop(1, n, go, 0)

    start_all(copy1)
    recv1[me] = send1[pl.ds(pl.multiple_of(me * step, step), wrows), :]
    wait_all(copy1, recv1, ss1, rs1)
    total = recv1[0]
    for s in range(1, n):
        total = total + recv1[s]
    sum1[...] = total
    fr_pad = wrows // groups
    for g in range(groups):
        win = sum1[pl.ds(g, fr_pad, stride=groups), :]
        win = jnp.concatenate([win, jnp.zeros((LANES - fr_pad, LANES), f32)], axis=0)
        place[g * LANES : (g + 1) * LANES, :] = win.T

    lane16 = lax.broadcasted_iota(jnp.int32, (lev, LANES), 1)
    tiles = table_hi.shape[0] // LANES
    x_tiles = []
    for t in range(tiles):
        acc = jnp.zeros((lev, LANES), f32)
        for j in range(per):
            k = t * per + j - 1
            if k > rows:
                break
            piece = place[slot[k] * lev : (slot[k] + 1) * lev, :]
            if j:
                piece = pltpu.roll(piece, j * frame, 1)
            acc = jnp.where((lane16 >= j * frame) & (lane16 < (j + 1) * frame), piece, acc)
        x_tiles.append(acc)
    x = jnp.concatenate(x_tiles, axis=1)
    x = jnp.concatenate([x, jnp.zeros((16 - lev, x.shape[1]), f32)], axis=0)
    x_hi = x.astype(bf16).astype(f32)
    x2 = jnp.concatenate([x_hi, x - x_hi], axis=0).astype(bf16)
    y = dims(x2, table_hi[...], 1, 0)
    y = y[0:16] + y[16:32] + dims(x_hi.astype(bf16), table_lo[...], 1, 0)

    state = back + y[0:lev, 0:cells]
    slope = y[0:lev, cells : 2 * cells] + back_slope
    factor = 1.0 - advect_rate * slope
    moved = state * factor
    adv_ref[:, 0, :] = moved
    cot = obs_a * moved - obs_b
    uv = jnp.concatenate([cot * factor, (-advect_rate) * (state * cot)], axis=1)
    uv = jnp.concatenate([uv, jnp.zeros((16 - lev, 2 * cells), f32)], axis=0)
    uv_hi = uv.astype(bf16).astype(f32)
    uv2 = jnp.concatenate([uv_hi, uv - uv_hi], axis=0).astype(bf16)
    gr = dims(uv2, table_hi[...], 1, 1)
    gr = gr[0:16] + gr[16:32] + dims(uv_hi.astype(bf16), table_lo[...], 1, 1)
    for t in range(tiles):
        tile = gr[0:lev, t * LANES : (t + 1) * LANES]
        for j in range(per):
            k = t * per + j - 1
            if k > rows:
                break
            piece = tile if j == 0 else pltpu.roll(tile, LANES - j * frame, 1)
            piece = jnp.where(lane16 < frame, piece, 0.0)
            frame_rows[slot[k] * lev : (slot[k] + 1) * lev, :] = piece

    start_band(frame_copy, frame_recv)
    wait_band(frame_copy)
    frame_rows[up_at : up_at + 2 * lev, :] += frame_recv[0]
    frame_rows[down_at : down_at + 2 * lev, :] += frame_recv[1]
    for g in range(groups):
        send2[pl.ds(g, fr_pad, stride=groups), :] = frame_rows[g * LANES : (g + 1) * LANES, :].T[0:fr_pad]
    start_all(copy2)
    recv2[me] = send2[...]
    wait_all(copy2, recv2, ss2, rs2)

    over = wrows - step
    for d in range(n):
        merged[d * step : (d + 1) * step, :] = recv2[d, 0:step, :]
    for d in range(n):
        e = (d + 1) % n
        merged[e * step : e * step + over, :] += recv2[d, step:wrows, :]
    for g in range(groups):
        for t in range(lon // LANES):
            piece = merged[pl.ds(groups * t * LANES + g, LANES, stride=groups), :].T
            coarse[g * LANES : (g + 1) * LANES, t * LANES : (t + 1) * LANES] = piece

    def weighted(k):
        cg = coarse[slot[k] * lev : (slot[k] + 1) * lev, :]
        return ens_row(k) * pltpu.roll(cg, lon - 1, 1) * scale

    a, b = weighted(-1), weighted(0)
    for k in range(rows):
        c = weighted(k + 1)
        z = smooth_lon(0.25 * a + 0.5 * b + 0.25 * c)
        for t in range(lon // LANES):
            grad_ref.at[t][pl.ds(k, lev, stride=rows), :] = z[:, t * LANES : (t + 1) * LANES]
        a, b = b, c


def up_to(x, m):
    return -(-x // m) * m


def to_tiles(x):
    return x.reshape(-1, x.shape[3] // LANES, LANES).swapaxes(0, 1)


def shards(ensemble, alpha, lat_lower, lat_weight, background, obs_cell, obs_value, obs_precision):
    n, nb = lax.axis_size("mem"), lax.axis_size("band")
    members, lev, rows, lon = ensemble.shape
    fine_rows = lat_lower.shape[0]
    cells = background.shape[2]
    scale = 1.0 / math.sqrt(members * n - 1)
    block = lon // n
    frame = block + 2
    groups = up_to((rows + 2) * lev, LANES) // LANES
    wrows = up_to(groups * frame, 8 * groups // math.gcd(8, groups))
    per = LANES // frame
    kaps = -(-(rows + 2) // per) * LANES
    cfg = (n, nb, lev, rows, lon, fine_rows, cells // fine_rows, scale)
    levp = up_to(lev, 8)
    dma = pltpu.SemaphoreType.DMA
    vm = pl.BlockSpec(memory_space=pltpu.VMEM)
    advected, gradient = pl.pallas_call(
        functools.partial(kernel, cfg),
        out_shape=(
            jax.ShapeDtypeStruct(background.shape, f32),
            jax.ShapeDtypeStruct((lon // LANES, lev * rows, LANES), f32),
        ),
        in_specs=[vm] * 8,
        out_specs=(vm, vm),
        scratch_shapes=[
            pltpu.VMEM((lon // LANES, lev * rows, LANES), f32),
            pltpu.VMEM((2, 3, levp, lon), f32),
            pltpu.VMEM((2, 3, levp, lon), f32),
            pltpu.VMEM((groups * LANES, lon), f32),
            pltpu.VMEM((groups * lon + wrows, LANES), f32),
            pltpu.VMEM((n, wrows, LANES), f32),
            pltpu.VMEM((wrows, LANES), f32),
            pltpu.VMEM((groups * LANES, LANES), f32),
            pltpu.VMEM((kaps, 2 * cells), bf16),
            pltpu.VMEM((kaps, 2 * cells), bf16),
            pltpu.VMEM((groups * LANES, LANES), f32),
            pltpu.VMEM((2, 2 * lev, LANES), f32),
            pltpu.VMEM((wrows, LANES), f32),
            pltpu.VMEM((n, wrows, LANES), f32),
            pltpu.VMEM((groups * lon, LANES), f32),
            pltpu.VMEM((groups * LANES, lon), f32),
            dma((2,)),
            dma((2,)),
            dma((2,)),
            dma((2,)),
            dma((n,)),
            dma((n,)),
            dma((n,)),
            dma((n,)),
            pltpu.VMEM((2,) + background.shape, f32),
            dma((2,)),
            dma((2,)),
        ],
        compiler_params=pltpu.CompilerParams(collective_id=0, has_side_effects=True, vmem_limit_bytes=48 * 2**20),
    )(
        to_tiles(ensemble),
        to_tiles(alpha),
        lat_lower.reshape(1, fine_rows),
        lat_weight.reshape(1, fine_rows),
        background,
        obs_cell,
        obs_value,
        obs_precision,
    )
    return advected, gradient.swapaxes(0, 1).reshape(members, lev, rows, lon)


def solution(mesh):
    return jax.shard_map(
        shards,
        mesh=mesh,
        in_specs=(
            P("mem", None, "band", None),
            P("mem", None, "band", None),
            P("band"),
            P("band"),
            P(None, ("band", "mem"), None),
            P(("band", "mem"), None),
            P(None, ("band", "mem"), None),
            P(("band", "mem"), None),
        ),
        out_specs=(P(None, ("band", "mem"), None), P("mem", None, "band", None)),
        check_vma=False,
    )
```

profile of v0, /device:TPU:0, one launch (start us, length us, event | category | flops | bytes accessed | tf_op | source)
XLA Modules:
  0.0 31.9 jit_solution(16420013504503717961)
XLA Ops:
  0.6 0.0 copy-start.5
  0.6 0.0 copy-start.7
  0.7 0.0 copy-start.4
  0.7 0.0 copy-start.6
  0.7 0.6 %copy-done.5 = f32[1,256]{1,0:T(1,128)S(1)} copy-done((f32[1,256]{1,0:T(1,128)S(1)}, f32[1,256]{1,0:T(1,128)}, u32[]{:S(2)}) %copy-start.5) | copy-done | bytes 1048
  1.3 0.0 copy-done.7
  1.3 0.0 copy-done.4
  1.3 0.0 copy-done.6
  1.3 0.0 copy-start
  1.3 0.9 %copy-done = f32[1,12,16,128]{3,2,1,0:T(8,128)S(1)} copy-done((f32[1,12,16,128]{3,2,1,0:T(8,128)S(1)}, f32[1,12,16,128]{3,2,1,0:T(8,128)}, u32[]{:S(2)}) %copy-start) | copy-done | bytes 98328
  2.2 0.0 copy-start.1
  2.2 0.8 %copy-done.1 = f32[12,1,1152]{2,1,0:T(1,128)S(1)} copy-done((f32[12,1,1152]{2,1,0:T(1,128)S(1)}, f32[12,1,1152]{2,1,0:T(1,128)}, u32[]{:S(2)}) %copy-start.1) | copy-done | bytes 55320
  3.1 0.0 copy-start.2
  3.1 0.8 %copy-done.2 = bf16[1,12,16,128]{3,2,1,0:T(8,128)(2,1)S(1)} copy-done((bf16[1,12,16,128]{3,2,1,0:T(8,128)(2,1)S(1)}, bf16[1,12,16,128]{3,2,1,0:T(8,128)(2,1)}, u32[]{:S(2)}) %copy-start.2) | copy-done | bytes 49176
  3.9 0.0 copy-start.3
  3.9 0.7 %copy-done.3 = f32[12,1,256]{2,1,0:T(1,128)S(1)} copy-done((f32[12,1,256]{2,1,0:T(1,128)S(1)}, f32[12,1,256]{2,1,0:T(1,128)}, u32[]{:S(2)}) %copy-start.3) | copy-done | bytes 12312
  4.6 26.1 %shard_map.95 = (f32[12,1,1152]{2,1,0:T(1,128)S(1)}, f32[1,192,128]{2,1,0:T(8,128)S(1)}) custom-call(bf16[1,192,128]{2,1,0:T(8,128)(2,1)S(1)} %bitcast.7, f32[1,192,128]{2,1,0:T(8,128)S(1)} %bitcast.5, s32[1,48]{1,0:T(1,128)S(1)} %bitcast.8, f32[1,48]{1,0:T(1,128)S(1)} %bitcast.9, f32[12,1,1152]{2,1,0:T(1,128)S(1)} %copy-done.1, s32[1,256]{1,0:T(1,128)S(1)} %copy-done.4, ...), custom_call_target="tpu_custom_call" | custom-call | tf_op jit(solution)/shard_map/pallas_call | solution.py:424
  30.6 0.6 %copy.12 = f32[12,1,1152]{2,1,0:T(1,128)} copy(f32[12,1,1152]{2,1,0:T(1,128)S(1)} %get-tuple-element.8) | data formatting | bytes 110592
  31.2 0.6 %copy.13 = f32[1,12,16,128]{3,2,1,0:T(8,128)} copy(f32[1,12,16,128]{3,2,1,0:T(8,128)S(1)} %bitcast.6) | data formatting | bytes 196608
Async XLA Ops:
  0.6 0.7 %copy-start.5 = (f32[1,256]{1,0:T(1,128)S(1)}, f32[1,256]{1,0:T(1,128)}, u32[]{:S(2)}) copy-start(f32[1,256]{1,0:T(1,128)} %prec_ref.1) | copy-start | bytes 3076
  0.6 0.7 %copy-start.7 = (f32[48]{0:T(128)S(1)}, f32[48]{0:T(128)}, u32[]{:S(2)}) copy-start(f32[48]{0:T(128)} %param.11) | copy-start | bytes 580
  0.7 0.7 %copy-start.4 = (s32[1,256]{1,0:T(1,128)S(1)}, s32[1,256]{1,0:T(1,128)}, u32[]{:S(2)}) copy-start(s32[1,256]{1,0:T(1,128)} %cell_ref.1) | copy-start | bytes 3076
  0.7 0.7 %copy-start.6 = (s32[48]{0:T(128)S(1)}, s32[48]{0:T(128)}, u32[]{:S(2)}) copy-start(s32[48]{0:T(128)} %param.10) | copy-start | bytes 580
  1.3 0.9 %copy-start = (f32[1,12,16,128]{3,2,1,0:T(8,128)S(1)}, f32[1,12,16,128]{3,2,1,0:T(8,128)}, u32[]{:S(2)}) copy-start(f32[1,12,16,128]{3,2,1,0:T(8,128)} %param.9) | copy-start | bytes 294916
  2.2 0.8 %copy-start.1 = (f32[12,1,1152]{2,1,0:T(1,128)S(1)}, f32[12,1,1152]{2,1,0:T(1,128)}, u32[]{:S(2)}) copy-start(f32[12,1,1152]{2,1,0:T(1,128)} %bg_ref.1) | copy-start | bytes 165892
  3.1 0.8 %copy-start.2 = (bf16[1,12,16,128]{3,2,1,0:T(8,128)(2,1)S(1)}, bf16[1,12,16,128]{3,2,1,0:T(8,128)(2,1)}, u32[]{:S(2)}) copy-start(bf16[1,12,16,128]{3,2,1,0:T(8,128)(2,1)} %param.8) | copy-start | bytes 147460
  3.9 0.7 %copy-start.3 = (f32[12,1,256]{2,1,0:T(1,128)S(1)}, f32[12,1,256]{2,1,0:T(1,128)}, u32[]{:S(2)}) copy-start(f32[12,1,256]{2,1,0:T(1,128)} %val_ref.1) | copy-start | bytes 36868
where the time goes:
time: 32.2 us; the launch traced here: 31.9 us
  Pallas kernels  26.1 us (81%)
  local copies, waits for them, and re-layouts  5.16 us (16%)
  between operations  0.68 us (2%)
    pallas_call x1, Pallas kernels, shards(): pl.pallas_call(functools.partial(kernel, cfg), out_shape=(jax.ShapeDtypeS...  26.1 us
    unnamed x18, local copies, waits for them, and re-layouts  5.16 us

commit v1 on v0

v1 whole, which is shorter than its diff:
```python
import functools
import math

import jax
import jax.numpy as jnp
from jax import lax
from jax.experimental import pallas as pl
from jax.experimental.pallas import tpu as pltpu
from jax.sharding import PartitionSpec as P

advect_rate = 0.25
LANES = 128
SUB = 8
RG = 16
f32 = jnp.float32
bf16 = jnp.bfloat16


def split2(x):
    hi = x.astype(bf16)
    lo = (x - hi.astype(f32)).astype(bf16)
    return hi, lo


def split2f(x):
    hi = x.astype(bf16).astype(f32)
    return hi, x - hi


def dims(a, b, ca, cb):
    return lax.dot_general(a, b, (((ca,), (cb,)), ((), ())), preferred_element_type=f32)


def iota(shape, d):
    return lax.broadcasted_iota(jnp.int32, shape, d)


def smooth_lon(x):
    n = x.shape[1]
    return 0.25 * pltpu.roll(x, 1, 1) + 0.5 * x + 0.25 * pltpu.roll(x, n - 1, 1)


def lon_weights(ratio):
    def parts(shift):
        num = 2 * shift + 1 + ratio
        return num // (2 * ratio), (num % (2 * ratio)) / (2 * ratio)

    def taps(shift):
        q, f = parts(shift)
        w = [0.0, 0.0, 0.0]
        for at, v in ((q, 1.0 - f), (q + 1, f)):
            if v:
                w[at] += v
        return w

    value = [taps(b) for b in range(ratio)]
    slope = [[0.5 * (p - m) for p, m in zip(taps(b + 1), taps(b - 1))] for b in range(ratio)]
    return value, slope


def combine(weights, parts):
    out = None
    for w, p in zip(weights, parts):
        if w == 0.0:
            continue
        term = p if w == 1.0 else w * p
        out = term if out is None else out + term
    return out


def kernel(
    cfg,
    ens_hbm,
    alpha_hbm,
    low_hbm,
    wt_hbm,
    bg_hbm,
    cell_hbm,
    val_hbm,
    prec_hbm,
    adv_ref,
    grad_ref,
    ens_in,
    alpha,
    low,
    wt,
    bg,
    cell,
    val,
    prec,
    ensf,
    plain,
    part,
    edge_send,
    edge_recv,
    send1,
    recv1,
    table_hi,
    table_lo,
    zbuf,
    rbuf,
    abuf,
    fine_bg,
    obs_a,
    obs_b,
    fe_send,
    fe_recv,
    lbuf,
    gbuf,
    advbuf,
    send2,
    recv2,
    recvx,
    merged,
    in_sem,
    edge_ss,
    edge_rs,
    ss1,
    rs1,
    fe_ss,
    fe_rs,
    ss2,
    rs2,
    ssx,
    rsx,
):
    n, nb, lev, rows, lon, fine_rows, fine_cols, scale = cfg
    block = lon // n
    frame = block + 2
    ratio = fine_cols // block
    main = lev * rows
    tiles = lon // LANES
    ng = fine_rows // RG
    gcells = RG * fine_cols
    gl = RG * RG
    levp = RG
    xs = recvx.shape[0]
    me = lax.axis_index("mem")
    band = lax.axis_index("band")
    has_up = band > 0
    has_down = band < nb - 1
    has = (has_up, has_down)
    wv, ws = lon_weights(ratio)

    barrier = pltpu.get_barrier_semaphore()

    def greet(o, c):
        pl.semaphore_signal(barrier, inc=1, device_id={"mem": lax.rem(me + o, n)})
        return c

    lax.fori_loop(1, n, greet, 0)

    @pl.when(has_up)
    def _():
        pl.semaphore_signal(barrier, inc=1, device_id={"band": band - 1})

    @pl.when(has_down)
    def _():
        pl.semaphore_signal(barrier, inc=1, device_id={"band": band + 1})

    loads = [
        pltpu.make_async_copy(src, dst, in_sem.at[i])
        for i, (src, dst) in enumerate(
            (
                (alpha_hbm, alpha),
                (ens_hbm, ens_in),
                (bg_hbm, bg),
                (low_hbm, low),
                (wt_hbm, wt),
                (cell_hbm, cell),
                (val_hbm, val),
                (prec_hbm, prec),
            )
        )
    ]
    for c in loads:
        c.start()

    for ref in (recv1, recv2, recvx):
        ref[:, :, frame:, :] = jnp.zeros(ref.shape[:2] + (ref.shape[2] - frame, LANES), f32)
    part[main:, :] = jnp.zeros((part.shape[0] - main, lon), f32)
    edge_send[...] = jnp.zeros(edge_send.shape, f32)
    fe_send[...] = jnp.zeros(fe_send.shape, f32)

    loads[0].wait()
    loads[1].wait()

    def whole(ref):
        parts = [ref[t] for t in range(tiles)]
        return parts[0] if tiles == 1 else jnp.concatenate(parts, axis=1)

    def row(ref, k):
        parts = [ref.at[t][pl.ds(k, lev, stride=rows), :] for t in range(tiles)]
        return parts[0] if tiles == 1 else jnp.concatenate(parts, axis=1)

    for t in range(tiles):
        ensf[t] = ens_in[t].astype(f32)
    al = whole(alpha)
    en = whole(ensf)
    kk = iota((main, lon), 0) % rows
    a_up = jnp.where(kk == 0, 0.0, pltpu.roll(al, 1, 0))
    a_dn = jnp.where(kk == rows - 1, 0.0, pltpu.roll(al, main - 1, 0))
    z = smooth_lon(0.25 * (a_up + a_dn) + 0.5 * al) * en * scale
    for t in range(tiles):
        plain[t] = z[:, t * LANES : (t + 1) * LANES]
    part[0:main, :] = z
    mine = []
    for side, k in ((0, 0), (1, rows - 1)):
        a_edge = smooth_lon(row(alpha, k)) * (0.25 * scale)
        e_edge = row(ensf, k)
        mine.append((a_edge, e_edge))
        edge_send[side, 0, 0:lev, :] = a_edge
        edge_send[side, 1, 0:lev, :] = e_edge
        edge_send[side, 2, 0:lev, :] = row(plain, k)

    def lay(g):
        block_rows = part[g * LANES : (g + 1) * LANES, :]
        block_rows = pltpu.roll(block_rows, 1, 1)
        for t in range(tiles):
            send1[g, t * LANES : (t + 1) * LANES, :] = block_rows[:, t * LANES : (t + 1) * LANES].T
        send1[g, lon : lon + SUB, :] = send1[g, 0:SUB, :]

    lay(0)

    if nb == 2:
        pl.semaphore_wait(barrier, n)
    else:
        pl.semaphore_wait(barrier, n - 1 + has_up.astype(jnp.int32) + has_down.astype(jnp.int32))

    def edge_copy(side):
        return pltpu.make_async_remote_copy(
            src_ref=edge_send.at[side],
            dst_ref=edge_recv.at[1 - side],
            send_sem=edge_ss.at[side],
            recv_sem=edge_rs.at[1 - side],
            device_id={"band": band - 1 if side == 0 else band + 1},
        )

    for side in (0, 1):

        @pl.when(has[side])
        def _():
            edge_copy(side).start()

        @pl.when(jnp.logical_not(has[side]))
        def _():
            edge_recv[side] = jnp.zeros(edge_recv.shape[1:], f32)
            if xs > 1:
                recvx[side, :, 0:frame, :] = jnp.zeros((n, frame, LANES), f32)

    def copy1(g, dst):
        return pltpu.make_async_remote_copy(
            src_ref=send1.at[g, pl.ds(pl.multiple_of(dst * block, block), frame), :],
            dst_ref=recv1.at[g, me, pl.ds(0, frame), :],
            send_sem=ss1.at[g, dst],
            recv_sem=rs1.at[g, me],
            device_id={"mem": dst},
        )

    def others(go):
        def step(o, c):
            go(lax.rem(me + o, n))
            return c

        lax.fori_loop(1, n, step, 0)

    def arrive1(g, src):
        got = recv1.at[g, src, pl.ds(0, frame), :]
        pltpu.make_async_copy(got, got, rs1.at[g, src]).wait()

    others(lambda d: copy1(0, d).start())

    loads[2].wait()
    row32 = iota((4 * SUB, gcells), 0)
    col_of = jnp.where(row32 < ratio * SUB, (row32 % SUB) * ratio + row32 // SUB, -1)
    pick = (iota((4 * SUB, gcells), 1) % fine_cols == col_of).astype(f32).astype(bf16)
    pick2 = jnp.concatenate([pick, pick], axis=1)
    in_row = iota((RG, gcells), 1) // fine_cols == iota((RG, gcells), 0)
    zbuf[main:, :] = jnp.zeros((gl - main, 2 * gcells), bf16)
    back = bg[:, 0, :]
    for g in range(ng):
        hi, lo = split2f(back[:, g * gcells : (g + 1) * gcells])
        for l in range(lev):
            at = slice(l * RG, (l + 1) * RG)
            zbuf[at, 0:gcells] = jnp.where(in_row, jnp.broadcast_to(hi[l : l + 1], (RG, gcells)), 0.0).astype(bf16)
            zbuf[at, gcells : 2 * gcells] = jnp.where(in_row, jnp.broadcast_to(lo[l : l + 1], (RG, gcells)), 0.0).astype(bf16)
        fine_bg[:, g * gl : (g + 1) * gl] = dims(pick2, zbuf[...], 1, 1)
    first = fine_bg[0:1, :]
    last = fine_bg[ratio * SUB - 1 : ratio * SUB, :]
    for t in range(ng * gl // LANES):
        fe_send[0, t : t + 1, :] = first[:, t * LANES : (t + 1) * LANES]
        fe_send[1, t : t + 1, :] = last[:, t * LANES : (t + 1) * LANES]

    def fe_copy(side):
        return pltpu.make_async_remote_copy(
            src_ref=fe_send.at[side],
            dst_ref=fe_recv.at[1 - side],
            send_sem=fe_ss.at[side],
            recv_sem=fe_rs.at[1 - side],
            device_id={"mem": lax.rem(me + (n - 1 if side == 0 else 1), n)},
        )

    fe_copy(0).start()
    fe_copy(1).start()

    for side in (0, 1):

        @pl.when(has[side])
        def _():
            pltpu.make_async_copy(edge_recv.at[side], edge_recv.at[side], edge_rs.at[side]).wait()

        a_edge, e_edge = mine[side]
        at = main + side * 2 * levp
        part[at : at + lev, :] = edge_recv[side, 2, 0:lev, :] + edge_recv[side, 1, 0:lev, :] * a_edge
        part[at + levp : at + levp + lev, :] = edge_recv[side, 0, 0:lev, :] * e_edge
    lay(1)
    others(lambda d: copy1(1, d).start())
    for g in (0, 1):
        recv1[g, me] = send1[g, pl.ds(pl.multiple_of(me * block, block), 2 * SUB), :]

    loads[3].wait()
    loads[4].wait()
    lane = iota((SUB, LANES), 1)

    def per_row(v):
        v = jnp.concatenate([v, jnp.zeros((1, LANES - fine_rows), f32)], axis=1)
        v = jnp.broadcast_to(v, (SUB, LANES))
        out = []
        for g in range(ng):
            r = v if g == 0 else pltpu.roll(v, LANES - g * RG, 1)
            r = jnp.where(lane < RG, r, 0.0)
            for s in (RG, 2 * RG, 4 * RG):
                r = r + pltpu.roll(r, s, 1)
            out += [r] * (gl // LANES)
        return jnp.concatenate(out, axis=1)[0:1]

    wide = ng * gl
    wl = per_row(wt[...])
    jl = iota((1, wide), 1) % gl
    key0 = per_row(low[...].astype(f32)) + ((jl // RG) * 64 + 1).astype(f32)
    key1 = key0 + 1.0
    w_hi, w_lo = split2f(wl)
    o_hi, o_lo = split2f(1.0 - wl)
    chunk = 2 * RG

    def table_step(i, c):
        kap = iota((chunk, 1), 0) + i * chunk
        e = kap - main
        es = e // levp
        ek = jnp.where(es == 0, -1, jnp.where(es == 1, 0, jnp.where(es == 2, rows, rows - 1)))
        l = jnp.where(e < 0, kap // rows, e % levp)
        k = jnp.where(e < 0, kap % rows, ek)
        key = jnp.where(l < lev, l * 64 + k + 1, -1).astype(f32)
        m0 = key == key0
        m1 = key == key1
        at = pl.ds(pl.multiple_of(i * chunk, chunk), chunk)
        table_hi[at, :] = jnp.where(m0, o_hi, jnp.where(m1, w_hi, 0.0)).astype(bf16)
        table_lo[at, :] = jnp.where(m0, o_lo, jnp.where(m1, w_lo, 0.0)).astype(bf16)
        return c

    lax.fori_loop(0, table_hi.shape[0] // chunk, table_step, 0)

    for i in (5, 6, 7):
        loads[i].wait()
    nobs = cell.shape[1]
    crow = cell[...] // fine_cols
    ccol = cell[...] % fine_cols
    r32 = iota((4 * SUB, nobs), 0)
    col_o = jnp.where(r32 < ratio * SUB, (r32 % SUB) * ratio + r32 // SUB, -1)
    hot = (col_o == ccol).astype(f32).astype(bf16)
    hot2 = jnp.concatenate([hot, hot], axis=1)
    pr = prec[...]
    p_hi, p_lo = split2f(pr)
    v_hi, v_lo = split2f(val[:, 0, :] * pr)
    rbuf[main:, :] = jnp.zeros((gl - main, 2 * nobs), bf16)
    for g in range(ng):
        at_row = iota((RG, nobs), 0) + g * RG == crow
        for l in range(lev):
            at = slice(l * RG, (l + 1) * RG)
            rbuf[at, 0:nobs] = jnp.where(at_row, jnp.broadcast_to(v_hi[l : l + 1], (RG, nobs)), 0.0).astype(bf16)
            rbuf[at, nobs : 2 * nobs] = jnp.where(at_row, jnp.broadcast_to(v_lo[l : l + 1], (RG, nobs)), 0.0).astype(bf16)
        obs_b[:, g * gl : (g + 1) * gl] = dims(hot2, rbuf[...], 1, 1)
        ph = jnp.where(at_row, jnp.broadcast_to(p_hi, (RG, nobs)), 0.0).astype(bf16)
        plo = jnp.where(at_row, jnp.broadcast_to(p_lo, (RG, nobs)), 0.0).astype(bf16)
        for j in range(LANES // RG):
            abuf[j * RG : (j + 1) * RG, 0:nobs] = ph
            abuf[j * RG : (j + 1) * RG, nobs : 2 * nobs] = plo
        oa = dims(hot2, abuf[...], 1, 1)
        for j in range(gl // LANES):
            obs_a[:, g * gl + j * LANES : g * gl + (j + 1) * LANES] = oa

    for side in (0, 1):
        pltpu.make_async_copy(fe_recv.at[side], fe_recv.at[side], fe_rs.at[side]).wait()
    nt = wide // LANES
    left = jnp.concatenate([fe_recv[0, t : t + 1, :] for t in range(nt)], axis=1)
    right = jnp.concatenate([fe_recv[1, t : t + 1, :] for t in range(nt)], axis=1)
    fb = [fine_bg[b * SUB : (b + 1) * SUB, :] for b in range(ratio)]
    arow = iota((SUB, wide), 0)
    before0 = jnp.where(arow == 0, left, pltpu.roll(fb[ratio - 1], 1, 0))
    after_last = jnp.where(arow == SUB - 1, right, pltpu.roll(fb[0], SUB - 1, 0))
    chain = [before0] + fb + [after_last]
    slope_bg = [0.5 * (chain[b + 2] - chain[b]) for b in range(ratio)]

    others(lambda s: arrive1(0, s))
    others(lambda s: arrive1(1, s))
    xg = []
    for g in (0, 1):
        total = recv1[g, 0]
        for s in range(1, n):
            total = total + recv1[g, s]
        xg.append(total)
    x = jnp.concatenate(xg, axis=1)
    x_hi, x_lo = split2f(x)
    x2 = jnp.concatenate([x_hi, x_lo], axis=0).astype(bf16)
    y = dims(x2, table_hi[...], 1, 0)
    y = y[0:16] + y[16:32] + dims(x_hi.astype(bf16), table_lo[...], 1, 0)
    lbuf[...] = y
    taps = [lbuf[d : d + SUB, :] for d in range(3)]

    us, vs, moved = [], [], []
    for b in range(ratio):
        state = fb[b] + combine(wv[b], taps)
        slope = slope_bg[b] + combine(ws[b], taps)
        factor = 1.0 - advect_rate * slope
        mv = state * factor
        at = slice(b * SUB, (b + 1) * SUB)
        cot = obs_a[at, :] * mv - obs_b[at, :]
        us.append(cot * factor)
        vs.append((-advect_rate) * (state * cot))
        moved.append(mv)
    gbuf[...] = jnp.zeros(gbuf.shape, f32)
    for d in range(3):
        t = combine([wv[b][d] for b in range(ratio)] + [ws[b][d] for b in range(ratio)], us + vs)
        gbuf[d : d + SUB, :] += t
    gl_v = gbuf[...]
    g_hi, g_lo = split2f(gl_v)
    g2 = jnp.concatenate([g_hi, g_lo], axis=0).astype(bf16)
    gr = dims(g2, table_hi[...], 1, 1)
    gr = gr[0:16] + gr[16:32] + dims(g_hi.astype(bf16), table_lo[...], 1, 1)
    for g in (0, 1):
        send2[g] = gr[:, g * LANES : (g + 1) * LANES]

    def copyx(side, dst):
        return pltpu.make_async_remote_copy(
            src_ref=send2.at[1, pl.ds(0, frame), :],
            dst_ref=recvx.at[0 if xs == 1 else 1 - side, me, pl.ds(0, frame), :],
            send_sem=ssx.at[side, dst],
            recv_sem=rsx.at[0 if xs == 1 else 1 - side, me],
            device_id={"mem": dst, "band": band - 1 if side == 0 else band + 1},
        )

    def copy2(g, dst):
        return pltpu.make_async_remote_copy(
            src_ref=send2.at[g, pl.ds(0, frame), :],
            dst_ref=recv2.at[g, me, pl.ds(0, frame), :],
            send_sem=ss2.at[g, dst],
            recv_sem=rs2.at[g, me],
            device_id={"mem": dst},
        )

    def everyone(go):
        def step(o, c):
            go(lax.rem(me + o, n))
            return c

        lax.fori_loop(0, n, step, 0)

    for side in (0, 1):

        @pl.when(has[side])
        def _():
            everyone(lambda d: copyx(side, d).start())

    def both(d):
        copy2(0, d).start()
        copy2(1, d).start()

    others(both)
    for g in (0, 1):
        recv2[g, me] = send2[g]

    advbuf[...] = jnp.concatenate(moved + [jnp.zeros((SUB, wide), f32)], axis=0)
    pickt = jnp.concatenate([pick, pick], axis=0)
    for g in range(ng):
        hi, lo = split2(advbuf[:, g * gl : g * gl + main])
        e = dims(jnp.concatenate([hi, lo], axis=0), pickt, 0, 0)
        for l in range(lev):
            v = jnp.where(in_row, e[l * RG : (l + 1) * RG], 0.0)
            adv_ref[l, :, g * gcells : (g + 1) * gcells] = jnp.sum(v, axis=0, keepdims=True)

    def arrive2(s):
        for g in (0, 1):
            got = recv2.at[g, s, pl.ds(0, frame), :]
            pltpu.make_async_copy(got, got, rs2.at[g, s]).wait()

    others(arrive2)
    for side in (0, 1):

        @pl.when(has[side])
        def _():
            def step(s):
                i = 0 if xs == 1 else side
                got = recvx.at[i, s, pl.ds(0, frame), :]
                pltpu.make_async_copy(got, got, rsx.at[i, s]).wait()

            everyone(step)

    over = iota((SUB, LANES), 0) < frame - block

    def gather(ref):
        for d in range(n):
            tail = jnp.where(over, ref[(d - 1) % n, SUB : 2 * SUB, :], 0.0)
            merged[d * SUB : (d + 1) * SUB, :] = ref[d, 0:SUB, :] + tail
        cols = [merged[t * LANES : (t + 1) * LANES, :].T for t in range(tiles)]
        cols = cols[0] if tiles == 1 else jnp.concatenate(cols, axis=1)
        return pltpu.roll(cols, lon - 1, 1)

    c0 = gather(recv2.at[0])
    c1 = gather(recv2.at[1])
    cx = [gather(recvx.at[i]) for i in range(xs)]
    cu, cd = cx[0], cx[-1]
    e0 = main - LANES
    coarse = jnp.concatenate([c0, c1[0:e0]], axis=0)
    en = whole(ensf)
    wm = en * coarse * scale
    w_up = jnp.where(kk == 0, 0.0, pltpu.roll(wm, 1, 0))
    w_dn = jnp.where(kk == rows - 1, 0.0, pltpu.roll(wm, main - 1, 0))
    zz = smooth_lon(0.25 * (w_up + w_dn) + 0.5 * wm)
    for t in range(tiles):
        grad_ref[t] = zz[:, t * LANES : (t + 1) * LANES]
    for side, k, k_in in ((0, 0, 1), (1, rows - 1, rows - 2)):
        src = (cu, cd)[side]
        mine_at = e0 + side * 2 * levp
        edge_at = e0 + (1 - side) * 2 * levp
        extra = jnp.where(has[side], src[edge_at : edge_at + lev], 0.0)
        halo = c1[mine_at : mine_at + lev] + jnp.where(has[side], src[edge_at + levp : edge_at + levp + lev], 0.0)
        we = row(ensf, k) * extra * scale
        wh = edge_recv[side, 1, 0:lev, :] * halo * scale
        z_edge = smooth_lon(0.5 * we + 0.25 * wh)
        z_in = smooth_lon(0.25 * we)
        for t in range(tiles):
            cut = slice(t * LANES, (t + 1) * LANES)
            grad_ref.at[t][pl.ds(k, lev, stride=rows), :] += z_edge[:, cut]
            grad_ref.at[t][pl.ds(k_in, lev, stride=rows), :] += z_in[:, cut]

    for side in (0, 1):
        fe_copy(side).wait_send()

        @pl.when(has[side])
        def _():
            edge_copy(side).wait_send()
            everyone(lambda d: copyx(side, d).wait_send())

    def sent(d):
        for g in (0, 1):
            copy1(g, d).wait_send()
            copy2(g, d).wait_send()

    others(sent)


def up_to(x, m):
    return -(-x // m) * m


def to_tiles(x):
    return x.reshape(-1, x.shape[3] // LANES, LANES).swapaxes(0, 1)


def shards(ensemble, alpha, lat_lower, lat_weight, background, obs_cell, obs_value, obs_precision):
    n, nb = lax.axis_size("mem"), lax.axis_size("band")
    members, lev, rows, lon = ensemble.shape
    fine_rows = lat_lower.shape[0]
    cells = background.shape[2]
    nobs = obs_cell.shape[1]
    fine_cols = cells // fine_rows
    scale = 1.0 / math.sqrt(members * n - 1)
    block = lon // n
    main = lev * rows
    kaps = main + 4 * RG
    assert members == 1 and block == SUB and rows == RG and lev <= RG and kaps == 2 * LANES
    assert fine_rows % RG == 0 and fine_cols % block == 0 and fine_cols // block == 3
    cfg = (n, nb, lev, rows, lon, fine_rows, fine_cols, scale)
    tiles = lon // LANES
    ng = fine_rows // RG
    gl = RG * RG
    wide = ng * gl
    gcells = RG * fine_cols
    xs = 1 if nb == 2 else 2
    dma = pltpu.SemaphoreType.DMA
    vm = pl.BlockSpec(memory_space=pltpu.VMEM)
    hbm = pl.BlockSpec(memory_space=pltpu.HBM)
    fr = 2 * SUB
    advected, gradient = pl.pallas_call(
        functools.partial(kernel, cfg),
        out_shape=(
            jax.ShapeDtypeStruct(background.shape, f32),
            jax.ShapeDtypeStruct((tiles, main, LANES), f32),
        ),
        in_specs=[hbm] * 8,
        out_specs=(vm, vm),
        scratch_shapes=[
            pltpu.VMEM((tiles, main, LANES), bf16),
            pltpu.VMEM((tiles, main, LANES), f32),
            pltpu.VMEM((1, fine_rows), jnp.int32),
            pltpu.VMEM((1, fine_rows), f32),
            pltpu.VMEM(background.shape, f32),
            pltpu.VMEM((1, nobs), jnp.int32),
            pltpu.VMEM(obs_value.shape, f32),
            pltpu.VMEM((1, nobs), f32),
            pltpu.VMEM((tiles, main, LANES), f32),
            pltpu.VMEM((tiles, main, LANES), f32),
            pltpu.VMEM((kaps, lon), f32),
            pltpu.VMEM((2, 3, RG, lon), f32),
            pltpu.VMEM((2, 3, RG, lon), f32),
            pltpu.VMEM((2, lon + SUB, LANES), f32),
            pltpu.VMEM((2, n, fr, LANES), f32),
            pltpu.VMEM((kaps, wide), bf16),
            pltpu.VMEM((kaps, wide), bf16),
            pltpu.VMEM((gl, 2 * gcells), bf16),
            pltpu.VMEM((gl, 2 * nobs), bf16),
            pltpu.VMEM((LANES, 2 * nobs), bf16),
            pltpu.VMEM((4 * SUB, wide), f32),
            pltpu.VMEM((4 * SUB, wide), f32),
            pltpu.VMEM((4 * SUB, wide), f32),
            pltpu.VMEM((2, SUB, LANES), f32),
            pltpu.VMEM((2, SUB, LANES), f32),
            pltpu.VMEM((fr, wide), f32),
            pltpu.VMEM((fr, wide), f32),
            pltpu.VMEM((4 * SUB, wide), f32),
            pltpu.VMEM((2, fr, LANES), f32),
            pltpu.VMEM((2, n, fr, LANES), f32),
            pltpu.VMEM((xs, n, fr, LANES), f32),
            pltpu.VMEM((lon, LANES), f32),
            dma((8,)),
            dma((2,)),
            dma((2,)),
            dma((2, n)),
            dma((2, n)),
            dma((2,)),
            dma((2,)),
            dma((2, n)),
            dma((2, n)),
            dma((2, n)),
            dma((xs, n)),
        ],
        compiler_params=pltpu.CompilerParams(collective_id=0, has_side_effects=True, vmem_limit_bytes=48 * 2**20),
    )(
        to_tiles(ensemble),
        to_tiles(alpha),
        lat_lower.reshape(1, fine_rows),
        lat_weight.reshape(1, fine_rows),
        background,
        obs_cell,
        obs_value,
        obs_precision,
    )
    return advected, gradient.swapaxes(0, 1).reshape(members, lev, rows, lon)


def solution(mesh):
    return jax.shard_map(
        shards,
        mesh=mesh,
        in_specs=(
            P("mem", None, "band", None),
            P("mem", None, "band", None),
            P("band"),
            P("band"),
            P(None, ("band", "mem"), None),
            P(("band", "mem"), None),
            P(None, ("band", "mem"), None),
            P(("band", "mem"), None),
        ),
        out_specs=(P(None, ("band", "mem"), None), P("mem", None, "band", None)),
        check_vma=False,
    )
```

time: 32.2 us -> 29.5 us (0.916)
  Pallas kernels: 26.1 us -> 23.4 us
    pallas_call x1, Pallas kernels: 26.1 us -> 23.4 us  [shards(): pl.pallas_call(functools.partial(kernel, cfg), out_shape=(jax.ShapeDtypeS...]
where the time goes in v1:
time: 29.5 us; the launch traced here: 29.2 us
  Pallas kernels  23.4 us (79%)
  local copies, waits for them, and re-layouts  5.16 us (17%)
  between operations  0.68 us (2%)
    pallas_call x1, Pallas kernels, shards(): pl.pallas_call(functools.partial(kernel, cfg), out_shape=(jax.ShapeDtypeS...  23.4 us
    unnamed x18, local copies, waits for them, and re-layouts  5.16 us

profile of v1, /device:TPU:0, one launch (start us, length us, event | category | flops | bytes accessed | tf_op | source)
XLA Modules:
  0.0 29.2 jit_solution(7218665600685306123)
XLA Ops:
  0.6 0.0 copy-start.5
  0.6 0.0 copy-start.7
  0.7 0.0 copy-start.4
  0.7 0.0 copy-start.6
  0.7 0.6 %copy-done.5 = f32[1,256]{1,0:T(1,128)S(1)} copy-done((f32[1,256]{1,0:T(1,128)S(1)}, f32[1,256]{1,0:T(1,128)}, u32[]{:S(2)}) %copy-start.5) | copy-done | bytes 1048
  1.3 0.0 copy-done.7
  1.3 0.0 copy-done.4
  1.3 0.0 copy-done.6
  1.3 0.0 copy-start
  1.3 0.9 %copy-done = f32[1,12,16,128]{3,2,1,0:T(8,128)S(1)} copy-done((f32[1,12,16,128]{3,2,1,0:T(8,128)S(1)}, f32[1,12,16,128]{3,2,1,0:T(8,128)}, u32[]{:S(2)}) %copy-start) | copy-done | bytes 98328
  2.2 0.0 copy-start.1
  2.2 0.8 %copy-done.1 = f32[12,1,1152]{2,1,0:T(1,128)S(1)} copy-done((f32[12,1,1152]{2,1,0:T(1,128)S(1)}, f32[12,1,1152]{2,1,0:T(1,128)}, u32[]{:S(2)}) %copy-start.1) | copy-done | bytes 55320
  3.1 0.0 copy-start.2
  3.1 0.8 %copy-done.2 = bf16[1,12,16,128]{3,2,1,0:T(8,128)(2,1)S(1)} copy-done((bf16[1,12,16,128]{3,2,1,0:T(8,128)(2,1)S(1)}, bf16[1,12,16,128]{3,2,1,0:T(8,128)(2,1)}, u32[]{:S(2)}) %copy-start.2) | copy-done | bytes 49176
  3.9 0.0 copy-start.3
  3.9 0.7 %copy-done.3 = f32[12,1,256]{2,1,0:T(1,128)S(1)} copy-done((f32[12,1,256]{2,1,0:T(1,128)S(1)}, f32[12,1,256]{2,1,0:T(1,128)}, u32[]{:S(2)}) %copy-start.3) | copy-done | bytes 12312
  4.6 23.4 %shard_map.95 = (f32[12,1,1152]{2,1,0:T(1,128)S(1)}, f32[1,192,128]{2,1,0:T(8,128)S(1)}) custom-call(bf16[1,192,128]{2,1,0:T(8,128)(2,1)S(1)} %bitcast.7, f32[1,192,128]{2,1,0:T(8,128)S(1)} %bitcast.5, s32[1,48]{1,0:T(1,128)S(1)} %bitcast.8, f32[1,48]{1,0:T(1,128)S(1)} %bitcast.9, f32[12,1,1152]{2,1,0:T(1,128)S(1)} %copy-done.1, s32[1,256]{1,0:T(1,128)S(1)} %copy-done.4, ...), custom_call_target="tpu_custom_call" | custom-call | tf_op jit(solution)/shard_map/pallas_call | solution.py:594
  28.0 0.6 %copy.12 = f32[12,1,1152]{2,1,0:T(1,128)} copy(f32[12,1,1152]{2,1,0:T(1,128)S(1)} %get-tuple-element.8) | data formatting | bytes 110592
  28.6 0.6 %copy.13 = f32[1,12,16,128]{3,2,1,0:T(8,128)} copy(f32[1,12,16,128]{3,2,1,0:T(8,128)S(1)} %bitcast.6) | data formatting | bytes 196608
Async XLA Ops:
  0.6 0.7 %copy-start.5 = (f32[1,256]{1,0:T(1,128)S(1)}, f32[1,256]{1,0:T(1,128)}, u32[]{:S(2)}) copy-start(f32[1,256]{1,0:T(1,128)} %prec_hbm.1) | copy-start | bytes 3076
  0.6 0.7 %copy-start.7 = (f32[48]{0:T(128)S(1)}, f32[48]{0:T(128)}, u32[]{:S(2)}) copy-start(f32[48]{0:T(128)} %param.11) | copy-start | bytes 580
  0.7 0.7 %copy-start.4 = (s32[1,256]{1,0:T(1,128)S(1)}, s32[1,256]{1,0:T(1,128)}, u32[]{:S(2)}) copy-start(s32[1,256]{1,0:T(1,128)} %cell_hbm.1) | copy-start | bytes 3076
  0.7 0.7 %copy-start.6 = (s32[48]{0:T(128)S(1)}, s32[48]{0:T(128)}, u32[]{:S(2)}) copy-start(s32[48]{0:T(128)} %param.10) | copy-start | bytes 580
  1.3 0.9 %copy-start = (f32[1,12,16,128]{3,2,1,0:T(8,128)S(1)}, f32[1,12,16,128]{3,2,1,0:T(8,128)}, u32[]{:S(2)}) copy-start(f32[1,12,16,128]{3,2,1,0:T(8,128)} %param.9) | copy-start | bytes 294916
  2.2 0.8 %copy-start.1 = (f32[12,1,1152]{2,1,0:T(1,128)S(1)}, f32[12,1,1152]{2,1,0:T(1,128)}, u32[]{:S(2)}) copy-start(f32[12,1,1152]{2,1,0:T(1,128)} %bg_hbm.1) | copy-start | bytes 165892
  3.1 0.8 %copy-start.2 = (bf16[1,12,16,128]{3,2,1,0:T(8,128)(2,1)S(1)}, bf16[1,12,16,128]{3,2,1,0:T(8,128)(2,1)}, u32[]{:S(2)}) copy-start(bf16[1,12,16,128]{3,2,1,0:T(8,128)(2,1)} %param.8) | copy-start | bytes 147460
  3.9 0.7 %copy-start.3 = (f32[12,1,256]{2,1,0:T(1,128)S(1)}, f32[12,1,256]{2,1,0:T(1,128)}, u32[]{:S(2)}) copy-start(f32[12,1,256]{2,1,0:T(1,128)} %val_hbm.1) | copy-start | bytes 36868

commit v2 on v1

--- a/solution.py
+++ b/solution.py
@@ -144,11 +144,8 @@
 
     barrier = pltpu.get_barrier_semaphore()
 
-    def greet(o, c):
+    for o in sorted(range(1, n), key=lambda o: -min(o, n - o)):
         pl.semaphore_signal(barrier, inc=1, device_id={"mem": lax.rem(me + o, n)})
-        return c
-
-    lax.fori_loop(1, n, greet, 0)
 
     @pl.when(has_up)
     def _():
@@ -252,8 +249,8 @@
         return pltpu.make_async_remote_copy(
             src_ref=send1.at[g, pl.ds(pl.multiple_of(dst * block, block), frame), :],
             dst_ref=recv1.at[g, me, pl.ds(0, frame), :],
-            send_sem=ss1.at[g, dst],
-            recv_sem=rs1.at[g, me],
+            send_sem=ss1.at[g],
+            recv_sem=rs1.at[g],
             device_id={"mem": dst},
         )
 
@@ -264,9 +261,9 @@
 
         lax.fori_loop(1, n, step, 0)
 
-    def arrive1(g, src):
-        got = recv1.at[g, src, pl.ds(0, frame), :]
-        pltpu.make_async_copy(got, got, rs1.at[g, src]).wait()
+    def all_of(ref, count, sem):
+        whole_ref = ref.at[pl.ds(0, count), pl.ds(0, frame), :]
+        pltpu.make_async_copy(whole_ref, whole_ref, sem).wait()
 
     others(lambda d: copy1(0, d).start())
 
@@ -401,8 +398,8 @@
     chain = [before0] + fb + [after_last]
     slope_bg = [0.5 * (chain[b + 2] - chain[b]) for b in range(ratio)]
 
-    others(lambda s: arrive1(0, s))
-    others(lambda s: arrive1(1, s))
+    for g in (0, 1):
+        all_of(recv1.at[g], n - 1, rs1.at[g])
     xg = []
     for g in (0, 1):
         total = recv1[g, 0]
@@ -444,8 +441,8 @@
         return pltpu.make_async_remote_copy(
             src_ref=send2.at[1, pl.ds(0, frame), :],
             dst_ref=recvx.at[0 if xs == 1 else 1 - side, me, pl.ds(0, frame), :],
-            send_sem=ssx.at[side, dst],
-            recv_sem=rsx.at[0 if xs == 1 else 1 - side, me],
+            send_sem=ssx.at[side],
+            recv_sem=rsx.at[0 if xs == 1 else 1 - side],
             device_id={"mem": dst, "band": band - 1 if side == 0 else band + 1},
         )
 
@@ -453,8 +450,8 @@
         return pltpu.make_async_remote_copy(
             src_ref=send2.at[g, pl.ds(0, frame), :],
             dst_ref=recv2.at[g, me, pl.ds(0, frame), :],
-            send_sem=ss2.at[g, dst],
-            recv_sem=rs2.at[g, me],
+            send_sem=ss2.at[g],
+            recv_sem=rs2.at[g],
             device_id={"mem": dst},
         )
 
@@ -488,22 +485,24 @@
             v = jnp.where(in_row, e[l * RG : (l + 1) * RG], 0.0)
             adv_ref[l, :, g * gcells : (g + 1) * gcells] = jnp.sum(v, axis=0, keepdims=True)
 
-    def arrive2(s):
-        for g in (0, 1):
-            got = recv2.at[g, s, pl.ds(0, frame), :]
-            pltpu.make_async_copy(got, got, rs2.at[g, s]).wait()
-
-    others(arrive2)
+    for g in (0, 1):
+        all_of(recv1.at[g], n - 1, ss1.at[g])
     for side in (0, 1):
+        fe_copy(side).wait_send()
 
         @pl.when(has[side])
         def _():
-            def step(s):
-                i = 0 if xs == 1 else side
-                got = recvx.at[i, s, pl.ds(0, frame), :]
-                pltpu.make_async_copy(got, got, rsx.at[i, s]).wait()
-
-            everyone(step)
+            edge_copy(side).wait_send()
+
+    for side in (0, 1):
+
+        @pl.when(has[side])
+        def _():
+            i = 0 if xs == 1 else side
+            all_of(recvx.at[i], n, rsx.at[i])
+
+    for g in (0, 1):
+        all_of(recv2.at[g], n - 1, rs2.at[g])
 
     over = iota((SUB, LANES), 0) < frame - block
 
@@ -544,19 +543,24 @@
             grad_ref.at[t][pl.ds(k_in, lev, stride=rows), :] += z_in[:, cut]
 
     for side in (0, 1):
-        fe_copy(side).wait_send()
 
         @pl.when(has[side])
         def _():
-            edge_copy(side).wait_send()
-            everyone(lambda d: copyx(side, d).wait_send())
-
-    def sent(d):
-        for g in (0, 1):
-            copy1(g, d).wait_send()
-            copy2(g, d).wait_send()
-
-    others(sent)
+            all_of(recvx.at[0], n, ssx.at[side])
+
+    for g in (0, 1):
+        all_of(recv2.at[g], n - 1, ss2.at[g])
+
+
+def writer(adv_ref, grad_ref, adv_out, grad_out, sem):
+    copies = [
+        pltpu.make_async_copy(grad_ref, grad_out, sem.at[0]),
+        pltpu.make_async_copy(adv_ref, adv_out, sem.at[1]),
+    ]
+    for c in copies:
+        c.start()
+    for c in copies:
+        c.wait()
 
 
 def up_to(x, m):
@@ -635,26 +639,42 @@
             dma((8,)),
             dma((2,)),
             dma((2,)),
-            dma((2, n)),
-            dma((2, n)),
-            dma((2,)),
-            dma((2,)),
-            dma((2, n)),
-            dma((2, n)),
-            dma((2, n)),
-            dma((xs, n)),
+            dma((2,)),
+            dma((2,)),
+            dma((2,)),
+            dma((2,)),
+            dma((2,)),
+            dma((2,)),
+            dma((2,)),
+            dma((xs,)),
         ],
         compiler_params=pltpu.CompilerParams(collective_id=0, has_side_effects=True, vmem_limit_bytes=48 * 2**20),
     )(
-        to_tiles(ensemble),
-        to_tiles(alpha),
-        lat_lower.reshape(1, fine_rows),
-        lat_weight.reshape(1, fine_rows),
-        background,
-        obs_cell,
-        obs_value,
-        obs_precision,
+        *(
+            pltpu.with_memory_space_constraint(v, pltpu.HBM)
+            for v in (
+                to_tiles(ensemble),
+                to_tiles(alpha),
+                lat_lower.reshape(1, fine_rows),
+                lat_weight.reshape(1, fine_rows),
+                background,
+                obs_cell,
+                obs_value,
+                obs_precision,
+            )
+        )
     )
+    advected, gradient = pl.pallas_call(
+        writer,
+        out_shape=(
+            jax.ShapeDtypeStruct(background.shape, f32),
+            jax.ShapeDtypeStruct((tiles, main, LANES), f32),
+        ),
+        in_specs=[vm, vm],
+        out_specs=(hbm, hbm),
+        scratch_shapes=[dma((2,))],
+        compiler_params=pltpu.CompilerParams(vmem_limit_bytes=2**20),
+    )(advected, gradient)
     return advected, gradient.swapaxes(0, 1).reshape(members, lev, rows, lon)
 
 

time: 29.5 us -> 23 us (0.78)
  local copies, waits for them, and re-layouts: 5.16 us -> 0 us
  Pallas kernels: 23.4 us -> 22.2 us
    unnamed x18 -> x0, local copies, waits for them, and re-layouts: 5.16 us -> none
    pallas_call x1, Pallas kernels: 23.4 us -> 21.6 us  [shards(): pl.pallas_call(functools.partial(kernel, cfg), out_shape=(jax.ShapeDtypeS...]
    pallas_call x0 -> x1, Pallas kernels: none -> 0.67 us  [shards(): pl.pallas_call(writer, out_shape=(jax.ShapeDtypeStruct(background.shape,...]
where the time goes in v2:
time: 23 us; the launch traced here: 22.9 us
  Pallas kernels  22.2 us (97%)
  between operations  0.64 us (3%)
    pallas_call x1, Pallas kernels, shards(): pl.pallas_call(functools.partial(kernel, cfg), out_shape=(jax.ShapeDtypeS...  21.6 us
    pallas_call x1, Pallas kernels, shards(): pl.pallas_call(writer, out_shape=(jax.ShapeDtypeStruct(background.shape,...  0.67 us

profile of v2, /device:TPU:0, one launch (start us, length us, event | category | flops | bytes accessed | tf_op | source)
XLA Modules:
  0.0 22.9 jit_solution(10707612110236514199)
XLA Ops:
  0.6 21.6 %shard_map.95 = (f32[12,1,1152]{2,1,0:T(1,128)S(1)}, f32[1,192,128]{2,1,0:T(8,128)S(1)}) custom-call(bf16[1,192,128]{2,1,0:T(8,128)(2,1)} %bitcast.6, f32[1,192,128]{2,1,0:T(8,128)} %bitcast.5, s32[1,48]{1,0:T(1,128)} %bitcast.7, f32[1,48]{1,0:T(1,128)} %bitcast.8, f32[12,1,1152]{2,1,0:T(1,128)} %bg_hbm.1, s32[1,256]{1,0:T(1,128)} %cell_hbm.1, ...), custom_call_target="tpu_custom_call" | custom-call | tf_op jit(solution)/shard_map/pallas_call | solution.py:598
  22.2 0.7 %shard_map.96 = (f32[12,1,1152]{2,1,0:T(1,128)}, f32[1,192,128]{2,1,0:T(8,128)}) custom-call(f32[12,1,1152]{2,1,0:T(1,128)S(1)} %get-tuple-element.6.adv_ref, f32[1,192,128]{2,1,0:T(8,128)S(1)} %get-tuple-element.7.grad_ref), custom_call_target="tpu_custom_call" | custom-call | tf_op jit(solution)/shard_map/pallas_call | solution.py:667

commit v3 on v2

--- a/solution.py
+++ b/solution.py
@@ -91,10 +91,18 @@
     ensf,
     plain,
     part,
+    xpart,
     edge_send,
     edge_recv,
-    send1,
+    flat,
+    frames,
+    pre_recv,
+    psum,
     recv1,
+    eloc,
+    rece,
+    ecr,
+    recc,
     table_hi,
     table_lo,
     zbuf,
@@ -110,19 +118,28 @@
     advbuf,
     send2,
     recv2,
+    sendx,
     recvx,
     merged,
     in_sem,
     edge_ss,
     edge_rs,
+    pre_ss,
+    pre_rs,
     ss1,
     rs1,
+    sse,
+    rse,
+    ssc,
+    rsc,
     fe_ss,
     fe_rs,
     ss2,
     rs2,
+    rs2f,
     ssx,
     rsx,
+    rsxf,
 ):
     n, nb, lev, rows, lon, fine_rows, fine_cols, scale = cfg
     block = lon // n
@@ -144,16 +161,21 @@
 
     barrier = pltpu.get_barrier_semaphore()
 
-    for o in sorted(range(1, n), key=lambda o: -min(o, n - o)):
+    core = lax.rem(me, 2)
+    chip = me // 2
+    partner = me + 1 - 2 * core
+    spread = sorted(range(n), key=lambda o: -min(o, n - o))
+    for side in (0, 1):
+
+        @pl.when(has[side])
+        def _():
+            for o in spread:
+                pl.semaphore_signal(
+                    barrier, inc=1, device_id={"mem": lax.rem(me + o, n), "band": band - 1 if side == 0 else band + 1}
+                )
+
+    for o in spread[:-1]:
         pl.semaphore_signal(barrier, inc=1, device_id={"mem": lax.rem(me + o, n)})
-
-    @pl.when(has_up)
-    def _():
-        pl.semaphore_signal(barrier, inc=1, device_id={"band": band - 1})
-
-    @pl.when(has_down)
-    def _():
-        pl.semaphore_signal(barrier, inc=1, device_id={"band": band + 1})
 
     loads = [
         pltpu.make_async_copy(src, dst, in_sem.at[i])
@@ -173,9 +195,8 @@
     for c in loads:
         c.start()
 
-    for ref in (recv1, recv2, recvx):
-        ref[:, :, frame:, :] = jnp.zeros(ref.shape[:2] + (ref.shape[2] - frame, LANES), f32)
     part[main:, :] = jnp.zeros((part.shape[0] - main, lon), f32)
+    xpart[...] = jnp.zeros(xpart.shape, f32)
     edge_send[...] = jnp.zeros(edge_send.shape, f32)
     fe_send[...] = jnp.zeros(fe_send.shape, f32)
 
@@ -201,28 +222,96 @@
     for t in range(tiles):
         plain[t] = z[:, t * LANES : (t + 1) * LANES]
     part[0:main, :] = z
-    mine = []
+    edges = []
     for side, k in ((0, 0), (1, rows - 1)):
         a_edge = smooth_lon(row(alpha, k)) * (0.25 * scale)
         e_edge = row(ensf, k)
-        mine.append((a_edge, e_edge))
-        edge_send[side, 0, 0:lev, :] = a_edge
-        edge_send[side, 1, 0:lev, :] = e_edge
-        edge_send[side, 2, 0:lev, :] = row(plain, k)
-
-    def lay(g):
-        block_rows = part[g * LANES : (g + 1) * LANES, :]
-        block_rows = pltpu.roll(block_rows, 1, 1)
+        edges.append((a_edge, e_edge, row(plain, k)))
+        edge_send[side, 0:lev, :] = e_edge
+        at = main + side * 2 * levp
+        part[at : at + lev, :] = a_edge
+        part[at + levp : at + levp + lev, :] = e_edge
+    (a_0, e_0, p_0), (a_1, e_1, p_1) = edges
+    zero = jnp.zeros_like(a_0)
+    sets_up = [p_0, zero, e_0, a_0]
+    sets_down = [e_1, a_1, p_1, zero]
+    if xs == 1:
+        sets = [jnp.where(has_up, u, d) for u, d in zip(sets_up, sets_down)]
+    else:
+        sets = sets_up + sets_down
+    for i, v in enumerate(sets):
+        xpart[i * levp : i * levp + lev, :] = v
+
+    def lay(g, rows_of):
+        rows_of = pltpu.roll(rows_of, 1, 1)
         for t in range(tiles):
-            send1[g, t * LANES : (t + 1) * LANES, :] = block_rows[:, t * LANES : (t + 1) * LANES].T
-        send1[g, lon : lon + SUB, :] = send1[g, 0:SUB, :]
-
-    lay(0)
+            flat[g, t * LANES : (t + 1) * LANES, :] = rows_of[:, t * LANES : (t + 1) * LANES].T
+        flat[g, lon : lon + SUB, :] = flat[g, 0:SUB, :]
+
+    lay(0, part[0:LANES, :])
+    lay(1, part[LANES : 2 * LANES, :])
+    lay(2, xpart[...])
+
+    lane8 = iota((SUB, LANES), 1)
+    row8 = iota((SUB, LANES), 0)
+    low_half = lane8 < LANES // 2
+    half = LANES // 2
+
+    def tile_of(g, d):
+        return flat[g, d * SUB : (d + 1) * SUB, :]
+
+    def views(d):
+        v, x = tile_of(1, d), tile_of(2, d)
+        flip, flipx = pltpu.roll(v, half, 1), pltpu.roll(x, half, 1)
+        return v, flip, x, flipx, pltpu.roll(flip, 5, 0), pltpu.roll(v, 3, 0), pltpu.roll(flipx, 3, 0), pltpu.roll(x, 3, 0)
+
+    cur = views(0)
+    for d in range(n):
+        nxt = views(d + 1)
+        v, flip, x, flipx, r5, v3, fx3, x3 = cur
+        packed = jnp.where(low_half, pltpu.roll(v, 2, 0), jnp.where(row8 < 5, r5, nxt[4]))
+        frames[d // 2, d % 2, 0:SUB, :] = tile_of(0, d)
+        frames[d // 2, d % 2, SUB : 2 * SUB, :] = jnp.where(row8 < 2, tile_of(0, d + 1), packed)
+        eloc[d] = jnp.where(low_half, flip, jnp.where(row8 < 3, v3, nxt[5]))
+        ecr[0, d] = jnp.where(low_half, x, jnp.where(row8 < 3, fx3, nxt[6]))
+        if xs == 2:
+            ecr[1, d] = jnp.where(low_half, flipx, jnp.where(row8 < 3, x3, nxt[7]))
+        cur = nxt
 
     if nb == 2:
-        pl.semaphore_wait(barrier, n)
+        pl.semaphore_wait(barrier, 2 * n - 1)
     else:
-        pl.semaphore_wait(barrier, n - 1 + has_up.astype(jnp.int32) + has_down.astype(jnp.int32))
+        pl.semaphore_wait(barrier, n - 1 + n * (has_up.astype(jnp.int32) + has_down.astype(jnp.int32)))
+
+    pre_copy = pltpu.make_async_remote_copy(
+        src_ref=frames.at[:, 1 - core],
+        dst_ref=pre_recv,
+        send_sem=pre_ss,
+        recv_sem=pre_rs,
+        device_id={"mem": partner},
+    )
+    pre_copy.start()
+    side_band = (band - 1, band + 1)
+    packed_rows = frame // 2
+
+    def copyc(side, dst):
+        i = 0 if xs == 1 else 1 - side
+        return pltpu.make_async_remote_copy(
+            src_ref=ecr.at[0 if xs == 1 else side, dst, pl.ds(0, packed_rows), :],
+            dst_ref=recc.at[i, me, pl.ds(0, packed_rows), :],
+            send_sem=ssc.at[side],
+            recv_sem=rsc.at[i],
+            device_id={"mem": dst, "band": side_band[side]},
+        )
+
+    def copye(dst):
+        return pltpu.make_async_remote_copy(
+            src_ref=eloc.at[dst, pl.ds(0, packed_rows), :],
+            dst_ref=rece.at[me, pl.ds(0, packed_rows), :],
+            send_sem=sse,
+            recv_sem=rse,
+            device_id={"mem": dst},
+        )
 
     def edge_copy(side):
         return pltpu.make_async_remote_copy(
@@ -230,42 +319,34 @@
             dst_ref=edge_recv.at[1 - side],
             send_sem=edge_ss.at[side],
             recv_sem=edge_rs.at[1 - side],
-            device_id={"band": band - 1 if side == 0 else band + 1},
-        )
-
+            device_id={"band": side_band[side]},
+        )
+
+    def go_round(first, go):
+        def step(o, c):
+            go(lax.rem(me + o, n))
+            return c
+
+        lax.fori_loop(first, n, step, 0)
+
+    for side in (0, 1):
+
+        @pl.when(has[side])
+        def _():
+            go_round(0, lambda d: copyc(side, d).start())
+
+        @pl.when(jnp.logical_not(has[side]))
+        def _():
+            edge_recv[side] = jnp.zeros(edge_recv.shape[1:], f32)
+
+    go_round(1, lambda d: copye(d).start())
     for side in (0, 1):
 
         @pl.when(has[side])
         def _():
             edge_copy(side).start()
 
-        @pl.when(jnp.logical_not(has[side]))
-        def _():
-            edge_recv[side] = jnp.zeros(edge_recv.shape[1:], f32)
-            if xs > 1:
-                recvx[side, :, 0:frame, :] = jnp.zeros((n, frame, LANES), f32)
-
-    def copy1(g, dst):
-        return pltpu.make_async_remote_copy(
-            src_ref=send1.at[g, pl.ds(pl.multiple_of(dst * block, block), frame), :],
-            dst_ref=recv1.at[g, me, pl.ds(0, frame), :],
-            send_sem=ss1.at[g],
-            recv_sem=rs1.at[g],
-            device_id={"mem": dst},
-        )
-
-    def others(go):
-        def step(o, c):
-            go(lax.rem(me + o, n))
-            return c
-
-        lax.fori_loop(1, n, step, 0)
-
-    def all_of(ref, count, sem):
-        whole_ref = ref.at[pl.ds(0, count), pl.ds(0, frame), :]
-        pltpu.make_async_copy(whole_ref, whole_ref, sem).wait()
-
-    others(lambda d: copy1(0, d).start())
+    rece[me] = eloc[me]
 
     loads[2].wait()
     row32 = iota((4 * SUB, gcells), 0)
@@ -300,20 +381,24 @@
     fe_copy(0).start()
     fe_copy(1).start()
 
-    for side in (0, 1):
-
-        @pl.when(has[side])
-        def _():
-            pltpu.make_async_copy(edge_recv.at[side], edge_recv.at[side], edge_rs.at[side]).wait()
-
-        a_edge, e_edge = mine[side]
-        at = main + side * 2 * levp
-        part[at : at + lev, :] = edge_recv[side, 2, 0:lev, :] + edge_recv[side, 1, 0:lev, :] * a_edge
-        part[at + levp : at + levp + lev, :] = edge_recv[side, 0, 0:lev, :] * e_edge
-    lay(1)
-    others(lambda d: copy1(1, d).start())
-    for g in (0, 1):
-        recv1[g, me] = send1[g, pl.ds(pl.multiple_of(me * block, block), 2 * SUB), :]
+    pre_copy.wait_recv()
+    for j in range(n // 2):
+        psum[j] = frames[j, core] + pre_recv[j]
+
+    used = frame + packed_rows
+
+    def copy1(dst):
+        return pltpu.make_async_remote_copy(
+            src_ref=psum.at[dst, pl.ds(0, used), :],
+            dst_ref=recv1.at[chip, pl.ds(0, used), :],
+            send_sem=ss1,
+            recv_sem=rs1,
+            device_id={"mem": 2 * dst + core},
+        )
+
+    for o in range(1, n // 2):
+        copy1(lax.rem(chip + o, n // 2)).start()
+    recv1[chip] = psum[chip]
 
     loads[3].wait()
     loads[4].wait()
@@ -398,15 +483,47 @@
     chain = [before0] + fb + [after_last]
     slope_bg = [0.5 * (chain[b + 2] - chain[b]) for b in range(ratio)]
 
-    for g in (0, 1):
-        all_of(recv1.at[g], n - 1, rs1.at[g])
-    xg = []
-    for g in (0, 1):
-        total = recv1[g, 0]
+    def all_of(ref, count, height, sem):
+        got = ref.at[pl.ds(0, count), pl.ds(0, height), :]
+        pltpu.make_async_copy(got, got, sem).wait()
+
+    all_of(rece, n - 1, packed_rows, rse)
+    for side in (0, 1):
+
+        @pl.when(has[side])
+        def _():
+            i = 0 if xs == 1 else side
+            all_of(recc.at[i], n, packed_rows, rsc.at[i])
+
+    prods, plains = [], []
+    for i in range(xs):
+        prod = rece[0] * recc[i, 0]
+        only = recc[i, 0]
         for s in range(1, n):
-            total = total + recv1[g, s]
-        xg.append(total)
-    x = jnp.concatenate(xg, axis=1)
+            prod = prod + rece[s] * recc[i, s]
+            only = only + recc[i, s]
+        prods.append(prod)
+        plains.append(only)
+    set_of = (lane8 % half) // levp
+    edge_sum = jnp.where(
+        set_of < 2, jnp.where(has_up, prods[0], 0.0), jnp.where(has_down, prods[-1], 0.0)
+    )
+    from_up = jnp.where(has_up, pltpu.roll(plains[0], LANES - 2 * levp, 1), 0.0)
+    from_down = jnp.where(has_down, pltpu.roll(plains[-1], 2 * levp, 1), 0.0)
+    edge_sum = edge_sum + jnp.where(set_of == 0, from_up, jnp.where(set_of == 2, from_down, 0.0))
+    edge_a = pltpu.roll(edge_sum, half, 1)
+    edge_b = pltpu.roll(edge_sum, 5, 0)
+
+    all_of(recv1, n // 2 - 1, used, rs1)
+    total = recv1[0]
+    for s in range(1, n // 2):
+        total = total + recv1[s]
+    m = total[SUB:]
+    m_a = pltpu.roll(m, SUB - 2, 0)
+    m_b = pltpu.roll(pltpu.roll(m, half, 1), 3, 0)
+    x_a = jnp.where(low_half, m_a, edge_a)
+    x_b = jnp.where(low_half, m_b, edge_b)
+    x = jnp.concatenate([total, jnp.concatenate([jnp.where(row8 < 5, x_a, x_b), x_b], axis=0)], axis=1)
     x_hi, x_lo = split2f(x)
     x2 = jnp.concatenate([x_hi, x_lo], axis=0).astype(bf16)
     y = dims(x2, table_hi[...], 1, 0)
@@ -436,45 +553,66 @@
     gr = gr[0:16] + gr[16:32] + dims(g_hi.astype(bf16), table_lo[...], 1, 1)
     for g in (0, 1):
         send2[g] = gr[:, g * LANES : (g + 1) * LANES]
+    v0, v1 = gr[0:SUB, LANES:], gr[SUB:, LANES:]
+    sendx[...] = jnp.where(
+        low_half, pltpu.roll(v0, half, 1), jnp.where(row8 < 3, pltpu.roll(v0, 3, 0), pltpu.roll(v1, 3, 0))
+    )
+
+    def slot2(src):
+        return recv2.at[src, :, pl.ds(0, frame), :]
+
+    def copy2(dst, sem):
+        return pltpu.make_async_remote_copy(
+            src_ref=send2.at[:, pl.ds(0, frame), :],
+            dst_ref=slot2(me),
+            send_sem=ss2,
+            recv_sem=sem,
+            device_id={"mem": dst},
+        )
+
+    def forward2(src):
+        return pltpu.make_async_remote_copy(
+            src_ref=slot2(src),
+            dst_ref=slot2(src),
+            send_sem=ss2,
+            recv_sem=rs2f,
+            device_id={"mem": partner},
+        )
+
+    def slotx(i, src):
+        return recvx.at[i, src, pl.ds(0, packed_rows), :]
 
     def copyx(side, dst):
+        i = 0 if xs == 1 else 1 - side
         return pltpu.make_async_remote_copy(
-            src_ref=send2.at[1, pl.ds(0, frame), :],
-            dst_ref=recvx.at[0 if xs == 1 else 1 - side, me, pl.ds(0, frame), :],
+            src_ref=sendx.at[pl.ds(0, packed_rows), :],
+            dst_ref=slotx(i, me),
             send_sem=ssx.at[side],
-            recv_sem=rsx.at[0 if xs == 1 else 1 - side],
-            device_id={"mem": dst, "band": band - 1 if side == 0 else band + 1},
-        )
-
-    def copy2(g, dst):
+            recv_sem=rsx.at[i, chip],
+            device_id={"mem": dst, "band": side_band[side]},
+        )
+
+    def forwardx(i, src):
         return pltpu.make_async_remote_copy(
-            src_ref=send2.at[g, pl.ds(0, frame), :],
-            dst_ref=recv2.at[g, me, pl.ds(0, frame), :],
-            send_sem=ss2.at[g],
-            recv_sem=rs2.at[g],
-            device_id={"mem": dst},
-        )
-
-    def everyone(go):
-        def step(o, c):
-            go(lax.rem(me + o, n))
-            return c
-
-        lax.fori_loop(0, n, step, 0)
+            src_ref=slotx(i, src),
+            dst_ref=slotx(i, src),
+            send_sem=ssx.at[2 + i],
+            recv_sem=rsxf.at[i],
+            device_id={"mem": partner},
+        )
 
     for side in (0, 1):
 
         @pl.when(has[side])
         def _():
-            everyone(lambda d: copyx(side, d).start())
-
-    def both(d):
-        copy2(0, d).start()
-        copy2(1, d).start()
-
-    others(both)
+            for o in range(0, n, 2):
+                copyx(side, lax.rem(me + o, n)).start()
+
+    for o in range(2, n, 2):
+        copy2(lax.rem(me + o, n), rs2.at[chip]).start()
+    copy2(partner, rs2f).start()
     for g in (0, 1):
-        recv2[g, me] = send2[g]
+        recv2[me, g] = send2[g]
 
     advbuf[...] = jnp.concatenate(moved + [jnp.zeros((SUB, wide), f32)], axis=0)
     pickt = jnp.concatenate([pick, pick], axis=0)
@@ -485,38 +623,72 @@
             v = jnp.where(in_row, e[l * RG : (l + 1) * RG], 0.0)
             adv_ref[l, :, g * gcells : (g + 1) * gcells] = jnp.sum(v, axis=0, keepdims=True)
 
-    for g in (0, 1):
-        all_of(recv1.at[g], n - 1, ss1.at[g])
-    for side in (0, 1):
-        fe_copy(side).wait_send()
-
-        @pl.when(has[side])
-        def _():
-            edge_copy(side).wait_send()
-
+    def sent_edges():
+        pre_copy.wait_send()
+        all_of(rece, n - 1, packed_rows, sse)
+        all_of(recv1, n // 2 - 1, used, ss1)
+        for side in (0, 1):
+            fe_copy(side).wait_send()
+
+            @pl.when(has[side])
+            def _():
+                all_of(recc.at[0], n, packed_rows, ssc.at[side])
+                edge_copy(side).wait_send()
+                pltpu.make_async_copy(edge_recv.at[side], edge_recv.at[side], edge_rs.at[side]).wait()
+
+    sent_edges()
+    for o in sorted(range(2, n, 2), key=lambda o: min(o, n - o)):
+        src = lax.rem(me + o, n)
+        pltpu.make_async_copy(slot2(src), slot2(src), rs2.at[src // 2]).wait()
+        forward2(src).start()
     for side in (0, 1):
 
         @pl.when(has[side])
         def _():
             i = 0 if xs == 1 else side
-            all_of(recvx.at[i], n, rsx.at[i])
-
-    for g in (0, 1):
-        all_of(recv2.at[g], n - 1, rs2.at[g])
+            for o in sorted(range(0, n, 2), key=lambda o: min(o, n - o)):
+                src = lax.rem(me + o, n)
+                pltpu.make_async_copy(slotx(i, src), slotx(i, src), rsx.at[i, src // 2]).wait()
+                forwardx(i, src).start()
+
+    def all_2(count, sem):
+        got = recv2.at[pl.ds(0, count), :, pl.ds(0, frame), :]
+        pltpu.make_async_copy(got, got, sem).wait()
+
+    for side in (0, 1):
+
+        @pl.when(has[side])
+        def _():
+            i = 0 if xs == 1 else side
+            all_of(recvx.at[i], n // 2, packed_rows, rsxf.at[i])
+
+    all_2(n // 2, rs2f)
 
     over = iota((SUB, LANES), 0) < frame - block
 
-    def gather(ref):
-        for d in range(n):
-            tail = jnp.where(over, ref[(d - 1) % n, SUB : 2 * SUB, :], 0.0)
-            merged[d * SUB : (d + 1) * SUB, :] = ref[d, 0:SUB, :] + tail
-        cols = [merged[t * LANES : (t + 1) * LANES, :].T for t in range(tiles)]
+    def across(ref):
+        cols = [ref[t * LANES : (t + 1) * LANES, :].T for t in range(tiles)]
         cols = cols[0] if tiles == 1 else jnp.concatenate(cols, axis=1)
         return pltpu.roll(cols, lon - 1, 1)
 
-    c0 = gather(recv2.at[0])
-    c1 = gather(recv2.at[1])
-    cx = [gather(recvx.at[i]) for i in range(xs)]
+    def gather(g):
+        for d in range(n):
+            tail = jnp.where(over, recv2[(d - 1) % n, g, SUB : 2 * SUB, :], 0.0)
+            merged[d * SUB : (d + 1) * SUB, :] = recv2[d, g, 0:SUB, :] + tail
+        return across(merged)
+
+    def gather_edges(i):
+        prev = pltpu.roll(pltpu.roll(recvx[i, n - 1], half, 1), 5, 0)
+        for d in range(n):
+            e = recvx[i, d]
+            b = pltpu.roll(pltpu.roll(e, half, 1), 5, 0)
+            merged[d * SUB : (d + 1) * SUB, :] = jnp.where(row8 < 5, e, b) + jnp.where(over, prev, 0.0)
+            prev = b
+        return across(merged)
+
+    c0 = gather(0)
+    c1 = gather(1)
+    cx = [gather_edges(i) for i in range(xs)]
     cu, cd = cx[0], cx[-1]
     e0 = main - LANES
     coarse = jnp.concatenate([c0, c1[0:e0]], axis=0)
@@ -530,11 +702,11 @@
     for side, k, k_in in ((0, 0, 1), (1, rows - 1, rows - 2)):
         src = (cu, cd)[side]
         mine_at = e0 + side * 2 * levp
-        edge_at = e0 + (1 - side) * 2 * levp
+        edge_at = (1 - side) * 2 * levp
         extra = jnp.where(has[side], src[edge_at : edge_at + lev], 0.0)
         halo = c1[mine_at : mine_at + lev] + jnp.where(has[side], src[edge_at + levp : edge_at + levp + lev], 0.0)
         we = row(ensf, k) * extra * scale
-        wh = edge_recv[side, 1, 0:lev, :] * halo * scale
+        wh = edge_recv[side, 0:lev, :] * halo * scale
         z_edge = smooth_lon(0.5 * we + 0.25 * wh)
         z_in = smooth_lon(0.25 * we)
         for t in range(tiles):
@@ -546,10 +718,11 @@
 
         @pl.when(has[side])
         def _():
-            all_of(recvx.at[0], n, ssx.at[side])
-
-    for g in (0, 1):
-        all_of(recv2.at[g], n - 1, ss2.at[g])
+            i = 0 if xs == 1 else side
+            all_of(recvx.at[0], n // 2, packed_rows, ssx.at[side])
+            all_of(recvx.at[0], n // 2, packed_rows, ssx.at[2 + i])
+
+    all_2(n - 1, ss2)
 
 
 def writer(adv_ref, grad_ref, adv_out, grad_out, sem):
@@ -582,7 +755,7 @@
     block = lon // n
     main = lev * rows
     kaps = main + 4 * RG
-    assert members == 1 and block == SUB and rows == RG and lev <= RG and kaps == 2 * LANES
+    assert n % 2 == 0 and members == 1 and block == SUB and rows == RG and lev <= RG and kaps == 2 * LANES
     assert fine_rows % RG == 0 and fine_cols % block == 0 and fine_cols // block == 3
     cfg = (n, nb, lev, rows, lon, fine_rows, fine_cols, scale)
     tiles = lon // LANES
@@ -615,10 +788,18 @@
             pltpu.VMEM((tiles, main, LANES), f32),
             pltpu.VMEM((tiles, main, LANES), f32),
             pltpu.VMEM((kaps, lon), f32),
-            pltpu.VMEM((2, 3, RG, lon), f32),
-            pltpu.VMEM((2, 3, RG, lon), f32),
-            pltpu.VMEM((2, lon + SUB, LANES), f32),
-            pltpu.VMEM((2, n, fr, LANES), f32),
+            pltpu.VMEM((LANES, lon), f32),
+            pltpu.VMEM((2, RG, lon), f32),
+            pltpu.VMEM((2, RG, lon), f32),
+            pltpu.VMEM((3, lon + SUB, LANES), f32),
+            pltpu.VMEM((n // 2, 2, fr, LANES), f32),
+            pltpu.VMEM((n // 2, fr, LANES), f32),
+            pltpu.VMEM((n // 2, fr, LANES), f32),
+            pltpu.VMEM((n // 2, fr, LANES), f32),
+            pltpu.VMEM((n, SUB, LANES), f32),
+            pltpu.VMEM((n, SUB, LANES), f32),
+            pltpu.VMEM((xs, n, SUB, LANES), f32),
+            pltpu.VMEM((xs, n, SUB, LANES), f32),
             pltpu.VMEM((kaps, wide), bf16),
             pltpu.VMEM((kaps, wide), bf16),
             pltpu.VMEM((gl, 2 * gcells), bf16),
@@ -633,19 +814,28 @@
             pltpu.VMEM((fr, wide), f32),
             pltpu.VMEM((4 * SUB, wide), f32),
             pltpu.VMEM((2, fr, LANES), f32),
-            pltpu.VMEM((2, n, fr, LANES), f32),
-            pltpu.VMEM((xs, n, fr, LANES), f32),
+            pltpu.VMEM((n, 2, fr, LANES), f32),
+            pltpu.VMEM((SUB, LANES), f32),
+            pltpu.VMEM((xs, n, SUB, LANES), f32),
             pltpu.VMEM((lon, LANES), f32),
             dma((8,)),
             dma((2,)),
             dma((2,)),
+            dma,
+            dma,
+            dma,
+            dma,
+            dma,
+            dma,
+            dma((2,)),
+            dma((xs,)),
             dma((2,)),
             dma((2,)),
-            dma((2,)),
-            dma((2,)),
-            dma((2,)),
-            dma((2,)),
-            dma((2,)),
+            dma,
+            dma((n // 2,)),
+            dma,
+            dma((4,)),
+            dma((xs, n // 2)),
             dma((xs,)),
         ],
         compiler_params=pltpu.CompilerParams(collective_id=0, has_side_effects=True, vmem_limit_bytes=48 * 2**20),

time: 23 us -> 21 us (0.913)
  the two profiles are of different devices: /device:TPU:0 before, /device:TPU:1 now
where the time goes in v3:
time: 21 us; the launch traced here: 20.8 us
  Pallas kernels  20.2 us (96%)
  between operations  0.64 us (3%)
    pallas_call x1, Pallas kernels, shards(): pl.pallas_call(functools.partial(kernel, cfg), out_shape=(jax.ShapeDtypeS...  19.5 us
    pallas_call x1, Pallas kernels, shards(): pl.pallas_call(writer, out_shape=(jax.ShapeDtypeStruct(background.shape,...  0.67 us

profile of v3, /device:TPU:1, one launch (start us, length us, event | category | flops | bytes accessed | tf_op | source)
XLA Modules:
  0.0 20.8 jit_solution(4499896539305045638)
XLA Ops:
  0.6 19.5 %shard_map.95 = (f32[12,1,1152]{2,1,0:T(1,128)S(1)}, f32[1,192,128]{2,1,0:T(8,128)S(1)}) custom-call(bf16[1,192,128]{2,1,0:T(8,128)(2,1)} %bitcast.6, f32[1,192,128]{2,1,0:T(8,128)} %bitcast.5, s32[1,48]{1,0:T(1,128)} %bitcast.7, f32[1,48]{1,0:T(1,128)} %bitcast.8, f32[12,1,1152]{2,1,0:T(1,128)} %bg_hbm.1, s32[1,256]{1,0:T(1,128)} %cell_hbm.1, ...), custom_call_target="tpu_custom_call" | custom-call | tf_op jit(solution)/shard_map/pallas_call | solution.py:771
  20.2 0.7 %shard_map.96 = (f32[12,1,1152]{2,1,0:T(1,128)}, f32[1,192,128]{2,1,0:T(8,128)}) custom-call(f32[12,1,1152]{2,1,0:T(1,128)S(1)} %get-tuple-element.6.adv_ref, f32[1,192,128]{2,1,0:T(8,128)S(1)} %get-tuple-element.7.grad_ref), custom_call_target="tpu_custom_call" | custom-call | tf_op jit(solution)/shard_map/pallas_call | solution.py:857

commit v4 on v3

--- a/solution.py
+++ b/solution.py
@@ -105,6 +105,8 @@
     recc,
     table_hi,
     table_lo,
+    back_hi,
+    back_lo,
     zbuf,
     rbuf,
     abuf,
@@ -122,17 +124,11 @@
     recvx,
     merged,
     in_sem,
-    edge_ss,
     edge_rs,
-    pre_ss,
     pre_rs,
-    ss1,
     rs1,
-    sse,
     rse,
-    ssc,
     rsc,
-    fe_ss,
     fe_rs,
     ss2,
     rs2,
@@ -165,17 +161,19 @@
     chip = me // 2
     partner = me + 1 - 2 * core
     spread = sorted(range(n), key=lambda o: -min(o, n - o))
-    for side in (0, 1):
-
-        @pl.when(has[side])
-        def _():
-            for o in spread:
-                pl.semaphore_signal(
-                    barrier, inc=1, device_id={"mem": lax.rem(me + o, n), "band": band - 1 if side == 0 else band + 1}
-                )
-
-    for o in spread[:-1]:
-        pl.semaphore_signal(barrier, inc=1, device_id={"mem": lax.rem(me + o, n)})
+    side_band = (band - 1, band + 1)
+    for o in spread:
+        if nb == 2:
+            pl.semaphore_signal(barrier, inc=1, device_id={"mem": lax.rem(me + o, n), "band": 1 - band})
+        else:
+            for side in (0, 1):
+
+                @pl.when(has[side])
+                def _():
+                    pl.semaphore_signal(barrier, inc=1, device_id={"mem": lax.rem(me + o, n), "band": side_band[side]})
+
+        if o:
+            pl.semaphore_signal(barrier, inc=1, device_id={"mem": lax.rem(me + o, n)})
 
     loads = [
         pltpu.make_async_copy(src, dst, in_sem.at[i])
@@ -278,76 +276,6 @@
             ecr[1, d] = jnp.where(low_half, flipx, jnp.where(row8 < 3, x3, nxt[7]))
         cur = nxt
 
-    if nb == 2:
-        pl.semaphore_wait(barrier, 2 * n - 1)
-    else:
-        pl.semaphore_wait(barrier, n - 1 + n * (has_up.astype(jnp.int32) + has_down.astype(jnp.int32)))
-
-    pre_copy = pltpu.make_async_remote_copy(
-        src_ref=frames.at[:, 1 - core],
-        dst_ref=pre_recv,
-        send_sem=pre_ss,
-        recv_sem=pre_rs,
-        device_id={"mem": partner},
-    )
-    pre_copy.start()
-    side_band = (band - 1, band + 1)
-    packed_rows = frame // 2
-
-    def copyc(side, dst):
-        i = 0 if xs == 1 else 1 - side
-        return pltpu.make_async_remote_copy(
-            src_ref=ecr.at[0 if xs == 1 else side, dst, pl.ds(0, packed_rows), :],
-            dst_ref=recc.at[i, me, pl.ds(0, packed_rows), :],
-            send_sem=ssc.at[side],
-            recv_sem=rsc.at[i],
-            device_id={"mem": dst, "band": side_band[side]},
-        )
-
-    def copye(dst):
-        return pltpu.make_async_remote_copy(
-            src_ref=eloc.at[dst, pl.ds(0, packed_rows), :],
-            dst_ref=rece.at[me, pl.ds(0, packed_rows), :],
-            send_sem=sse,
-            recv_sem=rse,
-            device_id={"mem": dst},
-        )
-
-    def edge_copy(side):
-        return pltpu.make_async_remote_copy(
-            src_ref=edge_send.at[side],
-            dst_ref=edge_recv.at[1 - side],
-            send_sem=edge_ss.at[side],
-            recv_sem=edge_rs.at[1 - side],
-            device_id={"band": side_band[side]},
-        )
-
-    def go_round(first, go):
-        def step(o, c):
-            go(lax.rem(me + o, n))
-            return c
-
-        lax.fori_loop(first, n, step, 0)
-
-    for side in (0, 1):
-
-        @pl.when(has[side])
-        def _():
-            go_round(0, lambda d: copyc(side, d).start())
-
-        @pl.when(jnp.logical_not(has[side]))
-        def _():
-            edge_recv[side] = jnp.zeros(edge_recv.shape[1:], f32)
-
-    go_round(1, lambda d: copye(d).start())
-    for side in (0, 1):
-
-        @pl.when(has[side])
-        def _():
-            edge_copy(side).start()
-
-    rece[me] = eloc[me]
-
     loads[2].wait()
     row32 = iota((4 * SUB, gcells), 0)
     col_of = jnp.where(row32 < ratio * SUB, (row32 % SUB) * ratio + row32 // SUB, -1)
@@ -363,6 +291,78 @@
             zbuf[at, 0:gcells] = jnp.where(in_row, jnp.broadcast_to(hi[l : l + 1], (RG, gcells)), 0.0).astype(bf16)
             zbuf[at, gcells : 2 * gcells] = jnp.where(in_row, jnp.broadcast_to(lo[l : l + 1], (RG, gcells)), 0.0).astype(bf16)
         fine_bg[:, g * gl : (g + 1) * gl] = dims(pick2, zbuf[...], 1, 1)
+    for c in loads[3:]:
+        c.wait()
+
+    if nb == 2:
+        pl.semaphore_wait(barrier, 2 * n - 1)
+    else:
+        pl.semaphore_wait(barrier, n - 1 + n * (has_up.astype(jnp.int32) + has_down.astype(jnp.int32)))
+
+    pre_copy = pltpu.make_async_remote_copy(
+        src_ref=frames.at[:, 1 - core],
+        dst_ref=pre_recv,
+        send_sem=in_sem.at[0],
+        recv_sem=pre_rs,
+        device_id={"mem": partner},
+    )
+    pre_copy.start()
+    packed_rows = frame // 2
+
+    def copyc(side, dst):
+        i = 0 if xs == 1 else 1 - side
+        return pltpu.make_async_remote_copy(
+            src_ref=ecr.at[0 if xs == 1 else side, dst, pl.ds(0, packed_rows), :],
+            dst_ref=recc.at[i, me, pl.ds(0, packed_rows), :],
+            send_sem=in_sem.at[2 + side],
+            recv_sem=rsc.at[i],
+            device_id={"mem": dst, "band": side_band[side]},
+        )
+
+    def copye(dst):
+        return pltpu.make_async_remote_copy(
+            src_ref=eloc.at[dst, pl.ds(0, packed_rows), :],
+            dst_ref=rece.at[me, pl.ds(0, packed_rows), :],
+            send_sem=in_sem.at[1],
+            recv_sem=rse,
+            device_id={"mem": dst},
+        )
+
+    def edge_copy(side):
+        return pltpu.make_async_remote_copy(
+            src_ref=edge_send.at[side],
+            dst_ref=edge_recv.at[1 - side],
+            send_sem=in_sem.at[6 + side],
+            recv_sem=edge_rs.at[0 if xs == 1 else 1 - side],
+            device_id={"band": side_band[side]},
+        )
+
+    def go_round(first, go):
+        def step(o, c):
+            go(lax.rem(me + o, n))
+            return c
+
+        lax.fori_loop(first, n, step, 0)
+
+    for side in (0, 1):
+
+        @pl.when(has[side])
+        def _():
+            go_round(0, lambda d: copyc(side, d).start())
+
+        @pl.when(jnp.logical_not(has[side]))
+        def _():
+            edge_recv[side] = jnp.zeros(edge_recv.shape[1:], f32)
+
+    go_round(1, lambda d: copye(d).start())
+    for side in (0, 1):
+
+        @pl.when(has[side])
+        def _():
+            edge_copy(side).start()
+
+    rece[me] = eloc[me]
+
     first = fine_bg[0:1, :]
     last = fine_bg[ratio * SUB - 1 : ratio * SUB, :]
     for t in range(ng * gl // LANES):
@@ -373,13 +373,77 @@
         return pltpu.make_async_remote_copy(
             src_ref=fe_send.at[side],
             dst_ref=fe_recv.at[1 - side],
-            send_sem=fe_ss.at[side],
-            recv_sem=fe_rs.at[1 - side],
+            send_sem=in_sem.at[5],
+            recv_sem=fe_rs,
             device_id={"mem": lax.rem(me + (n - 1 if side == 0 else 1), n)},
         )
 
     fe_copy(0).start()
     fe_copy(1).start()
+
+    lane = iota((SUB, LANES), 1)
+    wide = ng * gl
+
+    def per_row(v):
+        v = jnp.concatenate([v, jnp.zeros((1, LANES - fine_rows), f32)], axis=1)
+        return jnp.broadcast_to(v, (SUB, LANES))
+
+    def tiled(v, g):
+        r = v if g == 0 else pltpu.roll(v, LANES - g * RG, 1)
+        r = jnp.where(lane < RG, r, 0.0)
+        for s in (RG, 2 * RG, 4 * RG):
+            r = r + pltpu.roll(r, s, 1)
+        return jnp.concatenate([r, r], axis=0)
+
+    low_rows, wt_rows = per_row(low[...].astype(f32)), per_row(wt[...])
+    down = lambda v: jnp.concatenate([v] * (LANES // SUB), axis=0).T
+    low_col, wt_col = down(low_rows), down(wt_rows)
+    lane16 = iota((RG, LANES), 1)
+    row16 = iota((RG, LANES), 0)
+    lev_of = lane16 // RG
+    set_rows = (-1, 0, rows, rows - 1)
+    table_hi[...] = jnp.zeros(table_hi.shape, bf16)
+    table_lo[...] = jnp.zeros(table_lo.shape, bf16)
+    back_hi[...] = jnp.zeros(back_hi.shape, bf16)
+    back_lo[...] = jnp.zeros(back_lo.shape, bf16)
+    halves = gl // LANES
+    per = LANES // RG
+
+    def weigh(k, lo_k, w):
+        w_hi, w_lo = split2f(w)
+        o_hi, o_lo = split2f(1.0 - w)
+        m0, m1 = k == lo_k, k == lo_k + 1.0
+        return (
+            jnp.where(m0, o_hi, jnp.where(m1, w_hi, 0.0)),
+            jnp.where(m0, o_lo, jnp.where(m1, w_lo, 0.0)),
+        )
+
+    def put(ref, r, c, v, keep):
+        ref[r : r + RG, c : c + LANES] = jnp.where(keep, v, 0.0).astype(bf16)
+
+    for g in range(ng):
+        lo_t, w_t = tiled(low_rows, g), tiled(wt_rows, g)
+        main_t = weigh(row16.astype(f32), lo_t, w_t)
+        set_t = [weigh(jnp.full((RG, LANES), float(k), f32), lo_t, w_t) for k in set_rows]
+        for ref, which in ((table_hi, 0), (table_lo, 1)):
+            for l in range(lev):
+                put(ref, l * RG, g * gl + l // per * LANES, main_t[which], lev_of == l % per)
+            for s in range(4):
+                for h in range(halves):
+                    put(ref, main + s * levp, g * gl + h * LANES, set_t[s][which], (row16 == lev_of + h * per) & (row16 < lev))
+        lo_c, w_c = low_col[g * RG : (g + 1) * RG], wt_col[g * RG : (g + 1) * RG]
+        for h in range(halves):
+            kap = lane16 + h * LANES
+            e = kap - main
+            es = e // levp
+            ek = jnp.where(es == 0, -1, jnp.where(es == 1, 0, jnp.where(es == 2, rows, rows - 1)))
+            k_of = jnp.where(e < 0, kap % rows, ek).astype(f32)
+            l_of = jnp.where(e < 0, kap // rows, e % levp)
+            back_t = weigh(k_of, lo_c, w_c)
+            for ref, which in ((back_hi, 0), (back_lo, 1)):
+                for l in range(lev):
+                    if (h + 1) * LANES > main or l // per == h:
+                        put(ref, g * gl + l * RG, h * LANES, back_t[which], l_of == l)
 
     pre_copy.wait_recv()
     for j in range(n // 2):
@@ -391,7 +455,7 @@
         return pltpu.make_async_remote_copy(
             src_ref=psum.at[dst, pl.ds(0, used), :],
             dst_ref=recv1.at[chip, pl.ds(0, used), :],
-            send_sem=ss1,
+            send_sem=in_sem.at[4],
             recv_sem=rs1,
             device_id={"mem": 2 * dst + core},
         )
@@ -400,50 +464,6 @@
         copy1(lax.rem(chip + o, n // 2)).start()
     recv1[chip] = psum[chip]
 
-    loads[3].wait()
-    loads[4].wait()
-    lane = iota((SUB, LANES), 1)
-
-    def per_row(v):
-        v = jnp.concatenate([v, jnp.zeros((1, LANES - fine_rows), f32)], axis=1)
-        v = jnp.broadcast_to(v, (SUB, LANES))
-        out = []
-        for g in range(ng):
-            r = v if g == 0 else pltpu.roll(v, LANES - g * RG, 1)
-            r = jnp.where(lane < RG, r, 0.0)
-            for s in (RG, 2 * RG, 4 * RG):
-                r = r + pltpu.roll(r, s, 1)
-            out += [r] * (gl // LANES)
-        return jnp.concatenate(out, axis=1)[0:1]
-
-    wide = ng * gl
-    wl = per_row(wt[...])
-    jl = iota((1, wide), 1) % gl
-    key0 = per_row(low[...].astype(f32)) + ((jl // RG) * 64 + 1).astype(f32)
-    key1 = key0 + 1.0
-    w_hi, w_lo = split2f(wl)
-    o_hi, o_lo = split2f(1.0 - wl)
-    chunk = 2 * RG
-
-    def table_step(i, c):
-        kap = iota((chunk, 1), 0) + i * chunk
-        e = kap - main
-        es = e // levp
-        ek = jnp.where(es == 0, -1, jnp.where(es == 1, 0, jnp.where(es == 2, rows, rows - 1)))
-        l = jnp.where(e < 0, kap // rows, e % levp)
-        k = jnp.where(e < 0, kap % rows, ek)
-        key = jnp.where(l < lev, l * 64 + k + 1, -1).astype(f32)
-        m0 = key == key0
-        m1 = key == key1
-        at = pl.ds(pl.multiple_of(i * chunk, chunk), chunk)
-        table_hi[at, :] = jnp.where(m0, o_hi, jnp.where(m1, w_hi, 0.0)).astype(bf16)
-        table_lo[at, :] = jnp.where(m0, o_lo, jnp.where(m1, w_lo, 0.0)).astype(bf16)
-        return c
-
-    lax.fori_loop(0, table_hi.shape[0] // chunk, table_step, 0)
-
-    for i in (5, 6, 7):
-        loads[i].wait()
     nobs = cell.shape[1]
     crow = cell[...] // fine_cols
     ccol = cell[...] % fine_cols
@@ -471,8 +491,7 @@
         for j in range(gl // LANES):
             obs_a[:, g * gl + j * LANES : g * gl + (j + 1) * LANES] = oa
 
-    for side in (0, 1):
-        pltpu.make_async_copy(fe_recv.at[side], fe_recv.at[side], fe_rs.at[side]).wait()
+    pltpu.make_async_copy(fe_recv, fe_recv, fe_rs).wait()
     nt = wide // LANES
     left = jnp.concatenate([fe_recv[0, t : t + 1, :] for t in range(nt)], axis=1)
     right = jnp.concatenate([fe_recv[1, t : t + 1, :] for t in range(nt)], axis=1)
@@ -549,8 +568,8 @@
     gl_v = gbuf[...]
     g_hi, g_lo = split2f(gl_v)
     g2 = jnp.concatenate([g_hi, g_lo], axis=0).astype(bf16)
-    gr = dims(g2, table_hi[...], 1, 1)
-    gr = gr[0:16] + gr[16:32] + dims(g_hi.astype(bf16), table_lo[...], 1, 1)
+    gr = dims(g2, back_hi[...], 1, 0)
+    gr = gr[0:16] + gr[16:32] + dims(g_hi.astype(bf16), back_lo[...], 1, 0)
     for g in (0, 1):
         send2[g] = gr[:, g * LANES : (g + 1) * LANES]
     v0, v1 = gr[0:SUB, LANES:], gr[SUB:, LANES:]
@@ -579,24 +598,22 @@
             device_id={"mem": partner},
         )
 
-    def slotx(i, src):
-        return recvx.at[i, src, pl.ds(0, packed_rows), :]
-
     def copyx(side, dst):
         i = 0 if xs == 1 else 1 - side
         return pltpu.make_async_remote_copy(
             src_ref=sendx.at[pl.ds(0, packed_rows), :],
-            dst_ref=slotx(i, me),
-            send_sem=ssx.at[side],
-            recv_sem=rsx.at[i, chip],
+            dst_ref=recvx.at[i, core, chip, pl.ds(0, packed_rows), :],
+            send_sem=ssx.at[0 if xs == 1 else side],
+            recv_sem=rsx.at[i],
             device_id={"mem": dst, "band": side_band[side]},
         )
 
-    def forwardx(i, src):
+    def forwardx(i):
+        got = recvx.at[i, core, :, pl.ds(0, packed_rows), :]
         return pltpu.make_async_remote_copy(
-            src_ref=slotx(i, src),
-            dst_ref=slotx(i, src),
-            send_sem=ssx.at[2 + i],
+            src_ref=got,
+            dst_ref=got,
+            send_sem=ssx.at[xs + i],
             recv_sem=rsxf.at[i],
             device_id={"mem": partner},
         )
@@ -625,16 +642,16 @@
 
     def sent_edges():
         pre_copy.wait_send()
-        all_of(rece, n - 1, packed_rows, sse)
-        all_of(recv1, n // 2 - 1, used, ss1)
+        all_of(rece, n - 1, packed_rows, in_sem.at[1])
+        all_of(recv1, n // 2 - 1, used, in_sem.at[4])
+        pltpu.make_async_copy(fe_recv, fe_recv, in_sem.at[5]).wait()
         for side in (0, 1):
-            fe_copy(side).wait_send()
 
             @pl.when(has[side])
             def _():
-                all_of(recc.at[0], n, packed_rows, ssc.at[side])
+                all_of(recc.at[0], n, packed_rows, in_sem.at[2 + side])
                 edge_copy(side).wait_send()
-                pltpu.make_async_copy(edge_recv.at[side], edge_recv.at[side], edge_rs.at[side]).wait()
+                pltpu.make_async_copy(edge_recv.at[side], edge_recv.at[side], edge_rs.at[0 if xs == 1 else side]).wait()
 
     sent_edges()
     for o in sorted(range(2, n, 2), key=lambda o: min(o, n - o)):
@@ -646,10 +663,8 @@
         @pl.when(has[side])
         def _():
             i = 0 if xs == 1 else side
-            for o in sorted(range(0, n, 2), key=lambda o: min(o, n - o)):
-                src = lax.rem(me + o, n)
-                pltpu.make_async_copy(slotx(i, src), slotx(i, src), rsx.at[i, src // 2]).wait()
-                forwardx(i, src).start()
+            pltpu.make_async_copy(recvx.at[i, core, :, pl.ds(0, packed_rows), :], recvx.at[i, core, :, pl.ds(0, packed_rows), :], rsx.at[i]).wait()
+            forwardx(i).start()
 
     def all_2(count, sem):
         got = recv2.at[pl.ds(0, count), :, pl.ds(0, frame), :]
@@ -660,7 +675,7 @@
         @pl.when(has[side])
         def _():
             i = 0 if xs == 1 else side
-            all_of(recvx.at[i], n // 2, packed_rows, rsxf.at[i])
+            all_of(recvx.at[i, 0], n // 2, packed_rows, rsxf.at[i])
 
     all_2(n // 2, rs2f)
 
@@ -678,9 +693,9 @@
         return across(merged)
 
     def gather_edges(i):
-        prev = pltpu.roll(pltpu.roll(recvx[i, n - 1], half, 1), 5, 0)
+        prev = pltpu.roll(pltpu.roll(recvx[i, 1, n // 2 - 1], half, 1), 5, 0)
         for d in range(n):
-            e = recvx[i, d]
+            e = recvx[i, d % 2, d // 2]
             b = pltpu.roll(pltpu.roll(e, half, 1), 5, 0)
             merged[d * SUB : (d + 1) * SUB, :] = jnp.where(row8 < 5, e, b) + jnp.where(over, prev, 0.0)
             prev = b
@@ -719,8 +734,8 @@
         @pl.when(has[side])
         def _():
             i = 0 if xs == 1 else side
-            all_of(recvx.at[0], n // 2, packed_rows, ssx.at[side])
-            all_of(recvx.at[0], n // 2, packed_rows, ssx.at[2 + i])
+            all_of(recvx.at[0, 0], n // 2, packed_rows, ssx.at[i])
+            all_of(recvx.at[0, 0], n // 2, packed_rows, ssx.at[xs + i])
 
     all_2(n - 1, ss2)
 
@@ -802,6 +817,8 @@
             pltpu.VMEM((xs, n, SUB, LANES), f32),
             pltpu.VMEM((kaps, wide), bf16),
             pltpu.VMEM((kaps, wide), bf16),
+            pltpu.VMEM((wide, kaps), bf16),
+            pltpu.VMEM((wide, kaps), bf16),
             pltpu.VMEM((gl, 2 * gcells), bf16),
             pltpu.VMEM((gl, 2 * nobs), bf16),
             pltpu.VMEM((LANES, 2 * nobs), bf16),
@@ -816,26 +833,20 @@
             pltpu.VMEM((2, fr, LANES), f32),
             pltpu.VMEM((n, 2, fr, LANES), f32),
             pltpu.VMEM((SUB, LANES), f32),
-            pltpu.VMEM((xs, n, SUB, LANES), f32),
+            pltpu.VMEM((xs, 2, n // 2, SUB, LANES), f32),
             pltpu.VMEM((lon, LANES), f32),
             dma((8,)),
-            dma((2,)),
-            dma((2,)),
+            dma((xs,)),
             dma,
             dma,
             dma,
+            dma((xs,)),
             dma,
-            dma,
-            dma,
-            dma((2,)),
-            dma((xs,)),
-            dma((2,)),
-            dma((2,)),
             dma,
             dma((n // 2,)),
             dma,
-            dma((4,)),
-            dma((xs, n // 2)),
+            dma((2 * xs,)),
+            dma((xs,)),
             dma((xs,)),
         ],
         compiler_params=pltpu.CompilerParams(collective_id=0, has_side_effects=True, vmem_limit_bytes=48 * 2**20),

time: 21 us -> 20.7 us (0.986)
  Pallas kernels: 20.2 us -> 19.9 us
    pallas_call x1, Pallas kernels: 19.5 us -> 19.3 us  [shards(): pl.pallas_call(functools.partial(kernel, cfg), out_shape=(jax.ShapeDtypeS...]
where the time goes in v4:
time: 20.7 us; the launch traced here: 20.6 us
  Pallas kernels  19.9 us (96%)
  between operations  0.64 us (3%)
    pallas_call x1, Pallas kernels, shards(): pl.pallas_call(functools.partial(kernel, cfg), out_shape=(jax.ShapeDtypeS...  19.3 us
    pallas_call x1, Pallas kernels, shards(): pl.pallas_call(writer, out_shape=(jax.ShapeDtypeStruct(background.shape,...  0.67 us

profile of v4, /device:TPU:1, one launch (start us, length us, event | category | flops | bytes accessed | tf_op | source)
XLA Modules:
  0.0 20.6 jit_solution(10233419497042052905)
XLA Ops:
  0.6 19.3 %shard_map.95 = (f32[12,1,1152]{2,1,0:T(1,128)S(1)}, f32[1,192,128]{2,1,0:T(8,128)S(1)}) custom-call(bf16[1,192,128]{2,1,0:T(8,128)(2,1)} %bitcast.6, f32[1,192,128]{2,1,0:T(8,128)} %bitcast.5, s32[1,48]{1,0:T(1,128)} %bitcast.7, f32[1,48]{1,0:T(1,128)} %bitcast.8, f32[12,1,1152]{2,1,0:T(1,128)} %bg_hbm.1, s32[1,256]{1,0:T(1,128)} %cell_hbm.1, ...), custom_call_target="tpu_custom_call" | custom-call | tf_op jit(solution)/shard_map/pallas_call | solution.py:786
  19.9 0.7 %shard_map.96 = (f32[12,1,1152]{2,1,0:T(1,128)}, f32[1,192,128]{2,1,0:T(8,128)}) custom-call(f32[12,1,1152]{2,1,0:T(1,128)S(1)} %get-tuple-element.6.adv_ref, f32[1,192,128]{2,1,0:T(8,128)S(1)} %get-tuple-element.7.grad_ref), custom_call_target="tpu_custom_call" | custom-call | tf_op jit(solution)/shard_map/pallas_call | solution.py:868

commit v5 on v4

--- a/solution.py
+++ b/solution.py
@@ -66,6 +66,18 @@
         term = p if w == 1.0 else w * p
         out = term if out is None else out + term
     return out
+
+
+def chip_order(chips):
+    ring = 4 if chips % 4 == 0 else chips
+    rest = chips // ring
+
+    def hops(step):
+        return min(step[0], ring - step[0]) + min(step[1], rest - step[1])
+
+    steps = sorted(((a, b) for a in range(ring) for b in range(rest)), key=lambda s: -hops(s))
+    classes = [[s for s in steps if hops(s) == h] for h in sorted({hops(s) for s in steps if hops(s)}, reverse=True)]
+    return steps, classes, ring, rest
 
 
 def kernel(
@@ -160,20 +172,33 @@
     core = lax.rem(me, 2)
     chip = me // 2
     partner = me + 1 - 2 * core
-    spread = sorted(range(n), key=lambda o: -min(o, n - o))
+    chips = n // 2
+    far_first, classes, ring, rest = chip_order(chips)
+    ring_at, rest_at = chip // rest, lax.rem(chip, rest)
+
+    def to_chip(step):
+        return lax.rem(ring_at + step[0], ring) * rest + lax.rem(rest_at + step[1], rest)
+
+    def from_chip(step):
+        return to_chip(((ring - step[0]) % ring, (rest - step[1]) % rest))
+
     side_band = (band - 1, band + 1)
-    for o in spread:
-        if nb == 2:
-            pl.semaphore_signal(barrier, inc=1, device_id={"mem": lax.rem(me + o, n), "band": 1 - band})
-        else:
-            for side in (0, 1):
-
-                @pl.when(has[side])
-                def _():
-                    pl.semaphore_signal(barrier, inc=1, device_id={"mem": lax.rem(me + o, n), "band": side_band[side]})
-
-        if o:
-            pl.semaphore_signal(barrier, inc=1, device_id={"mem": lax.rem(me + o, n)})
+    for step in far_first:
+        home = step == (0, 0)
+        for c in (core, 1 - core):
+            if nb == 2:
+                pl.semaphore_signal(barrier, inc=1, device_id={"mem": 2 * to_chip(step) + c, "band": 1 - band})
+            else:
+                for side in (0, 1):
+
+                    @pl.when(has[side])
+                    def _():
+                        pl.semaphore_signal(
+                            barrier, inc=1, device_id={"mem": 2 * to_chip(step) + c, "band": side_band[side]}
+                        )
+
+            if not (home and c is core):
+                pl.semaphore_signal(barrier, inc=1, device_id={"mem": 2 * to_chip(step) + c})
 
     loads = [
         pltpu.make_async_copy(src, dst, in_sem.at[i])
@@ -337,24 +362,22 @@
             device_id={"band": side_band[side]},
         )
 
-    def go_round(first, go):
-        def step(o, c):
-            go(lax.rem(me + o, n))
-            return c
-
-        lax.fori_loop(first, n, step, 0)
-
     for side in (0, 1):
 
         @pl.when(has[side])
         def _():
-            go_round(0, lambda d: copyc(side, d).start())
+            for step in far_first:
+                for c in (core, 1 - core):
+                    copyc(side, 2 * to_chip(step) + c).start()
 
         @pl.when(jnp.logical_not(has[side]))
         def _():
             edge_recv[side] = jnp.zeros(edge_recv.shape[1:], f32)
 
-    go_round(1, lambda d: copye(d).start())
+    for step in far_first:
+        for c in (core, 1 - core):
+            if step != (0, 0) or c is not core:
+                copye(2 * to_chip(step) + c).start()
     for side in (0, 1):
 
         @pl.when(has[side])
@@ -460,8 +483,8 @@
             device_id={"mem": 2 * dst + core},
         )
 
-    for o in range(1, n // 2):
-        copy1(lax.rem(chip + o, n // 2)).start()
+    for step in far_first[:-1]:
+        copy1(to_chip(step)).start()
     recv1[chip] = psum[chip]
 
     nobs = cell.shape[1]
@@ -622,11 +645,12 @@
 
         @pl.when(has[side])
         def _():
-            for o in range(0, n, 2):
-                copyx(side, lax.rem(me + o, n)).start()
-
-    for o in range(2, n, 2):
-        copy2(lax.rem(me + o, n), rs2.at[chip]).start()
+            for step in far_first:
+                copyx(side, 2 * to_chip(step) + core).start()
+
+    for i, group in enumerate(classes):
+        for step in group:
+            copy2(2 * to_chip(step) + core, rs2.at[len(classes) - 1 - i]).start()
     copy2(partner, rs2f).start()
     for g in (0, 1):
         recv2[me, g] = send2[g]
@@ -654,10 +678,14 @@
                 pltpu.make_async_copy(edge_recv.at[side], edge_recv.at[side], edge_rs.at[0 if xs == 1 else side]).wait()
 
     sent_edges()
-    for o in sorted(range(2, n, 2), key=lambda o: min(o, n - o)):
-        src = lax.rem(me + o, n)
-        pltpu.make_async_copy(slot2(src), slot2(src), rs2.at[src // 2]).wait()
-        forward2(src).start()
+    def all_2(count, sem):
+        got = recv2.at[pl.ds(0, count), :, pl.ds(0, frame), :]
+        pltpu.make_async_copy(got, got, sem).wait()
+
+    for i, group in enumerate(reversed(classes)):
+        all_2(len(group), rs2.at[i])
+        for step in group:
+            forward2(2 * from_chip(step) + core).start()
     for side in (0, 1):
 
         @pl.when(has[side])
@@ -665,17 +693,6 @@
             i = 0 if xs == 1 else side
             pltpu.make_async_copy(recvx.at[i, core, :, pl.ds(0, packed_rows), :], recvx.at[i, core, :, pl.ds(0, packed_rows), :], rsx.at[i]).wait()
             forwardx(i).start()
-
-    def all_2(count, sem):
-        got = recv2.at[pl.ds(0, count), :, pl.ds(0, frame), :]
-        pltpu.make_async_copy(got, got, sem).wait()
-
-    for side in (0, 1):
-
-        @pl.when(has[side])
-        def _():
-            i = 0 if xs == 1 else side
-            all_of(recvx.at[i, 0], n // 2, packed_rows, rsxf.at[i])
 
     all_2(n // 2, rs2f)
 
@@ -703,8 +720,6 @@
 
     c0 = gather(0)
     c1 = gather(1)
-    cx = [gather_edges(i) for i in range(xs)]
-    cu, cd = cx[0], cx[-1]
     e0 = main - LANES
     coarse = jnp.concatenate([c0, c1[0:e0]], axis=0)
     en = whole(ensf)
@@ -714,6 +729,15 @@
     zz = smooth_lon(0.25 * (w_up + w_dn) + 0.5 * wm)
     for t in range(tiles):
         grad_ref[t] = zz[:, t * LANES : (t + 1) * LANES]
+    for side in (0, 1):
+
+        @pl.when(has[side])
+        def _():
+            i = 0 if xs == 1 else side
+            all_of(recvx.at[i, 0], n // 2, packed_rows, rsxf.at[i])
+
+    cx = [gather_edges(i) for i in range(xs)]
+    cu, cd = cx[0], cx[-1]
     for side, k, k_in in ((0, 0, 1), (1, rows - 1, rows - 2)):
         src = (cu, cd)[side]
         mine_at = e0 + side * 2 * levp
@@ -843,7 +867,7 @@
             dma((xs,)),
             dma,
             dma,
-            dma((n // 2,)),
+            dma((len(chip_order(n // 2)[1]),)),
             dma,
             dma((2 * xs,)),
             dma((xs,)),

time: 20.7 us -> 20.6 us (level)
  no operation moved by 1% of the time
where the time goes in v5:
time: 20.6 us; the launch traced here: 20.5 us
  Pallas kernels  19.8 us (96%)
  between operations  0.64 us (3%)
    pallas_call x1, Pallas kernels, shards(): pl.pallas_call(functools.partial(kernel, cfg), out_shape=(jax.ShapeDtypeS...  19.2 us
    pallas_call x1, Pallas kernels, shards(): pl.pallas_call(writer, out_shape=(jax.ShapeDtypeStruct(background.shape,...  0.67 us

profile of v5, /device:TPU:1, one launch (start us, length us, event | category | flops | bytes accessed | tf_op | source)
XLA Modules:
  0.0 20.5 jit_solution(3079932246289281504)
XLA Ops:
  0.6 19.2 %shard_map.95 = (f32[12,1,1152]{2,1,0:T(1,128)S(1)}, f32[1,192,128]{2,1,0:T(8,128)S(1)}) custom-call(bf16[1,192,128]{2,1,0:T(8,128)(2,1)} %bitcast.6, f32[1,192,128]{2,1,0:T(8,128)} %bitcast.5, s32[1,48]{1,0:T(1,128)} %bitcast.7, f32[1,48]{1,0:T(1,128)} %bitcast.8, f32[12,1,1152]{2,1,0:T(1,128)} %bg_hbm.1, s32[1,256]{1,0:T(1,128)} %cell_hbm.1, ...), custom_call_target="tpu_custom_call" | custom-call | tf_op jit(solution)/shard_map/pallas_call | solution.py:810
  19.8 0.7 %shard_map.96 = (f32[12,1,1152]{2,1,0:T(1,128)}, f32[1,192,128]{2,1,0:T(8,128)}) custom-call(f32[12,1,1152]{2,1,0:T(1,128)S(1)} %get-tuple-element.6.adv_ref, f32[1,192,128]{2,1,0:T(8,128)S(1)} %get-tuple-element.7.grad_ref), custom_call_target="tpu_custom_call" | custom-call | tf_op jit(solution)/shard_map/pallas_call | solution.py:892

commit v6 on v5

--- a/solution.py
+++ b/solution.py
@@ -135,6 +135,7 @@
     sendx,
     recvx,
     merged,
+    ensr,
     in_sem,
     edge_rs,
     pre_rs,
@@ -252,11 +253,11 @@
         edges.append((a_edge, e_edge, row(plain, k)))
         edge_send[side, 0:lev, :] = e_edge
         at = main + side * 2 * levp
-        part[at : at + lev, :] = a_edge
-        part[at + levp : at + levp + lev, :] = e_edge
+        for i, v in enumerate((a_edge, e_edge) if side == 0 else (e_edge, a_edge)):
+            part[at + i * levp : at + i * levp + lev, :] = v
     (a_0, e_0, p_0), (a_1, e_1, p_1) = edges
     zero = jnp.zeros_like(a_0)
-    sets_up = [p_0, zero, e_0, a_0]
+    sets_up = [zero, p_0, a_0, e_0]
     sets_down = [e_1, a_1, p_1, zero]
     if xs == 1:
         sets = [jnp.where(has_up, u, d) for u, d in zip(sets_up, sets_down)]
@@ -424,7 +425,7 @@
     lane16 = iota((RG, LANES), 1)
     row16 = iota((RG, LANES), 0)
     lev_of = lane16 // RG
-    set_rows = (-1, 0, rows, rows - 1)
+    set_rows = (-1, 0, rows - 1, rows)
     table_hi[...] = jnp.zeros(table_hi.shape, bf16)
     table_lo[...] = jnp.zeros(table_lo.shape, bf16)
     back_hi[...] = jnp.zeros(back_hi.shape, bf16)
@@ -459,7 +460,7 @@
             kap = lane16 + h * LANES
             e = kap - main
             es = e // levp
-            ek = jnp.where(es == 0, -1, jnp.where(es == 1, 0, jnp.where(es == 2, rows, rows - 1)))
+            ek = jnp.where(es == 0, -1, jnp.where(es == 1, 0, jnp.where(es == 2, rows - 1, rows)))
             k_of = jnp.where(e < 0, kap % rows, ek).astype(f32)
             l_of = jnp.where(e < 0, kap // rows, e % levp)
             back_t = weigh(k_of, lo_c, w_c)
@@ -552,7 +553,7 @@
     )
     from_up = jnp.where(has_up, pltpu.roll(plains[0], LANES - 2 * levp, 1), 0.0)
     from_down = jnp.where(has_down, pltpu.roll(plains[-1], 2 * levp, 1), 0.0)
-    edge_sum = edge_sum + jnp.where(set_of == 0, from_up, jnp.where(set_of == 2, from_down, 0.0))
+    edge_sum = edge_sum + jnp.where(set_of == 0, from_up, jnp.where(set_of == 3, from_down, 0.0))
     edge_a = pltpu.roll(edge_sum, half, 1)
     edge_b = pltpu.roll(edge_sum, 5, 0)
 
@@ -596,9 +597,23 @@
     for g in (0, 1):
         send2[g] = gr[:, g * LANES : (g + 1) * LANES]
     v0, v1 = gr[0:SUB, LANES:], gr[SUB:, LANES:]
-    sendx[...] = jnp.where(
-        low_half, pltpu.roll(v0, half, 1), jnp.where(row8 < 3, pltpu.roll(v0, 3, 0), pltpu.roll(v1, 3, 0))
-    )
+    quarter = lane8 // (2 * levp)
+    v32, v96, w32, w96 = (pltpu.roll(v, r, 1) for v in (v0, v1) for r in (2 * levp, 6 * levp))
+
+    def late(a, b):
+        return jnp.where(row8 < 3, pltpu.roll(a, 3, 0), pltpu.roll(b, 3, 0))
+
+    def pack_for(up_there):
+        near = jnp.where(up_there, v32, v96)
+        rest_cols = late(jnp.where(up_there, v96, v32), jnp.where(up_there, w96, w32))
+        q = jnp.where(up_there, quarter - 1, quarter)
+        return jnp.where(q == 2, near, jnp.where(q == 0, rest_cols, 0.0))
+
+    if xs == 1:
+        sendx[0] = pack_for(has_up)
+    else:
+        for side in (0, 1):
+            sendx[side] = pack_for(side == 0)
 
     def slot2(src):
         return recv2.at[src, :, pl.ds(0, frame), :]
@@ -624,7 +639,7 @@
     def copyx(side, dst):
         i = 0 if xs == 1 else 1 - side
         return pltpu.make_async_remote_copy(
-            src_ref=sendx.at[pl.ds(0, packed_rows), :],
+            src_ref=sendx.at[0 if xs == 1 else side, pl.ds(0, packed_rows), :],
             dst_ref=recvx.at[i, core, chip, pl.ds(0, packed_rows), :],
             send_sem=ssx.at[0 if xs == 1 else side],
             recv_sem=rsx.at[i],
@@ -682,6 +697,13 @@
         got = recv2.at[pl.ds(0, count), :, pl.ds(0, frame), :]
         pltpu.make_async_copy(got, got, sem).wait()
 
+    ensr[...] = pltpu.roll(whole(ensf), 1, 1) * scale
+    edge_ens = [pltpu.roll(row(ensf, k), 1, 1) * scale for k in (0, rows - 1)]
+    halo_ens = [pltpu.roll(edge_recv[side, 0:lev, :], 1, 1) * scale for side in (0, 1)]
+
+    def smooth_back(v):
+        return 0.25 * v + 0.5 * pltpu.roll(v, lon - 1, 1) + 0.25 * pltpu.roll(v, lon - 2, 1)
+
     for i, group in enumerate(reversed(classes)):
         all_2(len(group), rs2.at[i])
         for step in group:
@@ -700,35 +722,35 @@
 
     def across(ref):
         cols = [ref[t * LANES : (t + 1) * LANES, :].T for t in range(tiles)]
-        cols = cols[0] if tiles == 1 else jnp.concatenate(cols, axis=1)
-        return pltpu.roll(cols, lon - 1, 1)
+        return cols[0] if tiles == 1 else jnp.concatenate(cols, axis=1)
+
+    ours = (quarter < 2) | (set_of == 0) | (set_of == 3)
+    set_lanes = lane8 >= half
+
+    def edges_at(i, d):
+        e = recvx[i, d % 2, d // 2]
+        b = pltpu.roll(pltpu.roll(e, half, 1), 5, 0)
+        return jnp.where(row8 < 5, e, b), jnp.where(over, b, 0.0)
 
     def gather(g):
+        sides = range(xs) if g else ()
+        prev = [edges_at(i, n - 1)[1] for i in sides]
         for d in range(n):
-            tail = jnp.where(over, recv2[(d - 1) % n, g, SUB : 2 * SUB, :], 0.0)
-            merged[d * SUB : (d + 1) * SUB, :] = recv2[d, g, 0:SUB, :] + tail
-        return across(merged)
-
-    def gather_edges(i):
-        prev = pltpu.roll(pltpu.roll(recvx[i, 1, n // 2 - 1], half, 1), 5, 0)
-        for d in range(n):
-            e = recvx[i, d % 2, d // 2]
-            b = pltpu.roll(pltpu.roll(e, half, 1), 5, 0)
-            merged[d * SUB : (d + 1) * SUB, :] = jnp.where(row8 < 5, e, b) + jnp.where(over, prev, 0.0)
-            prev = b
-        return across(merged)
+            tile = recv2[d, g, 0:SUB, :] + jnp.where(over, recv2[(d - 1) % n, g, SUB : 2 * SUB, :], 0.0)
+            if g:
+                theirs = None
+                for i in sides:
+                    here, tail = edges_at(i, d)
+                    v = here + prev[i]
+                    if xs == 2:
+                        v = jnp.where(has[i], v, 0.0)
+                    theirs = v if theirs is None else theirs + v
+                    prev[i] = tail
+                tile = jnp.where(ours, tile, 0.0) + jnp.where(set_lanes, theirs, 0.0)
+            merged[g, d * SUB : (d + 1) * SUB, :] = tile
+        return across(merged.at[g])
 
     c0 = gather(0)
-    c1 = gather(1)
-    e0 = main - LANES
-    coarse = jnp.concatenate([c0, c1[0:e0]], axis=0)
-    en = whole(ensf)
-    wm = en * coarse * scale
-    w_up = jnp.where(kk == 0, 0.0, pltpu.roll(wm, 1, 0))
-    w_dn = jnp.where(kk == rows - 1, 0.0, pltpu.roll(wm, main - 1, 0))
-    zz = smooth_lon(0.25 * (w_up + w_dn) + 0.5 * wm)
-    for t in range(tiles):
-        grad_ref[t] = zz[:, t * LANES : (t + 1) * LANES]
     for side in (0, 1):
 
         @pl.when(has[side])
@@ -736,18 +758,21 @@
             i = 0 if xs == 1 else side
             all_of(recvx.at[i, 0], n // 2, packed_rows, rsxf.at[i])
 
-    cx = [gather_edges(i) for i in range(xs)]
-    cu, cd = cx[0], cx[-1]
+    c1 = gather(1)
+    e0 = main - LANES
+    coarse = jnp.concatenate([c0, c1[0:e0]], axis=0)
+    wm = ensr[...] * coarse
+    w_up = jnp.where(kk == 0, 0.0, pltpu.roll(wm, 1, 0))
+    w_dn = jnp.where(kk == rows - 1, 0.0, pltpu.roll(wm, main - 1, 0))
+    zz = smooth_back(0.25 * (w_up + w_dn) + 0.5 * wm)
+    for t in range(tiles):
+        grad_ref[t] = zz[:, t * LANES : (t + 1) * LANES]
     for side, k, k_in in ((0, 0, 1), (1, rows - 1, rows - 2)):
-        src = (cu, cd)[side]
-        mine_at = e0 + side * 2 * levp
-        edge_at = (1 - side) * 2 * levp
-        extra = jnp.where(has[side], src[edge_at : edge_at + lev], 0.0)
-        halo = c1[mine_at : mine_at + lev] + jnp.where(has[side], src[edge_at + levp : edge_at + levp + lev], 0.0)
-        we = row(ensf, k) * extra * scale
-        wh = edge_recv[side, 0:lev, :] * halo * scale
-        z_edge = smooth_lon(0.5 * we + 0.25 * wh)
-        z_in = smooth_lon(0.25 * we)
+        halo_at, extra_at = (e0, e0 + levp) if side == 0 else (e0 + 3 * levp, e0 + 2 * levp)
+        we = edge_ens[side] * c1[extra_at : extra_at + lev]
+        wh = halo_ens[side] * c1[halo_at : halo_at + lev]
+        z_edge = smooth_back(0.5 * we + 0.25 * wh)
+        z_in = smooth_back(0.25 * we)
         for t in range(tiles):
             cut = slice(t * LANES, (t + 1) * LANES)
             grad_ref.at[t][pl.ds(k, lev, stride=rows), :] += z_edge[:, cut]
@@ -856,9 +881,10 @@
             pltpu.VMEM((4 * SUB, wide), f32),
             pltpu.VMEM((2, fr, LANES), f32),
             pltpu.VMEM((n, 2, fr, LANES), f32),
-            pltpu.VMEM((SUB, LANES), f32),
+            pltpu.VMEM((xs, SUB, LANES), f32),
             pltpu.VMEM((xs, 2, n // 2, SUB, LANES), f32),
-            pltpu.VMEM((lon, LANES), f32),
+            pltpu.VMEM((2, lon, LANES), f32),
+            pltpu.VMEM((main, lon), f32),
             dma((8,)),
             dma((xs,)),
             dma,

time: 20.6 us -> 20.4 us (level)
  the two profiles are of different devices: /device:TPU:1 before, /device:TPU:0 now
where the time goes in v6:
time: 20.4 us; the launch traced here: 20.1 us
  Pallas kernels  19.4 us (95%)
  between operations  0.64 us (3%)
    pallas_call x1, Pallas kernels, shards(): pl.pallas_call(functools.partial(kernel, cfg), out_shape=(jax.ShapeDtypeS...  18.7 us
    pallas_call x1, Pallas kernels, shards(): pl.pallas_call(writer, out_shape=(jax.ShapeDtypeStruct(background.shape,...  0.67 us

profile of v6, /device:TPU:0, one launch (start us, length us, event | category | flops | bytes accessed | tf_op | source)
XLA Modules:
  0.0 20.1 jit_solution(1830609937544010504)
XLA Ops:
  0.6 18.7 %shard_map.95 = (f32[12,1,1152]{2,1,0:T(1,128)S(1)}, f32[1,192,128]{2,1,0:T(8,128)S(1)}) custom-call(bf16[1,192,128]{2,1,0:T(8,128)(2,1)} %bitcast.6, f32[1,192,128]{2,1,0:T(8,128)} %bitcast.5, s32[1,48]{1,0:T(1,128)} %bitcast.7, f32[1,48]{1,0:T(1,128)} %bitcast.8, f32[12,1,1152]{2,1,0:T(1,128)} %bg_hbm.1, s32[1,256]{1,0:T(1,128)} %cell_hbm.1, ...), custom_call_target="tpu_custom_call" | custom-call | tf_op jit(solution)/shard_map/pallas_call | solution.py:835
  19.4 0.7 %shard_map.96 = (f32[12,1,1152]{2,1,0:T(1,128)}, f32[1,192,128]{2,1,0:T(8,128)}) custom-call(f32[12,1,1152]{2,1,0:T(1,128)S(1)} %get-tuple-element.6.adv_ref, f32[1,192,128]{2,1,0:T(8,128)S(1)} %get-tuple-element.7.grad_ref), custom_call_target="tpu_custom_call" | custom-call | tf_op jit(solution)/shard_map/pallas_call | solution.py:918

commit v7 on v6

--- a/solution.py
+++ b/solution.py
@@ -127,14 +127,12 @@
     obs_b,
     fe_send,
     fe_recv,
-    lbuf,
-    gbuf,
     advbuf,
     send2,
     recv2,
     sendx,
     recvx,
-    merged,
+    ebuf,
     ensr,
     in_sem,
     edge_rs,
@@ -571,8 +569,7 @@
     x2 = jnp.concatenate([x_hi, x_lo], axis=0).astype(bf16)
     y = dims(x2, table_hi[...], 1, 0)
     y = y[0:16] + y[16:32] + dims(x_hi.astype(bf16), table_lo[...], 1, 0)
-    lbuf[...] = y
-    taps = [lbuf[d : d + SUB, :] for d in range(3)]
+    taps = [y[0:SUB]] + [pltpu.roll(y, 2 * SUB - d, 0)[0:SUB] for d in (1, 2)]
 
     us, vs, moved = [], [], []
     for b in range(ratio):
@@ -585,36 +582,17 @@
         us.append(cot * factor)
         vs.append((-advect_rate) * (state * cot))
         moved.append(mv)
-    gbuf[...] = jnp.zeros(gbuf.shape, f32)
+    gl_v = None
     for d in range(3):
         t = combine([wv[b][d] for b in range(ratio)] + [ws[b][d] for b in range(ratio)], us + vs)
-        gbuf[d : d + SUB, :] += t
-    gl_v = gbuf[...]
+        t = jnp.concatenate([t, jnp.zeros_like(t)], axis=0)
+        gl_v = t if d == 0 else gl_v + pltpu.roll(t, d, 0)
     g_hi, g_lo = split2f(gl_v)
     g2 = jnp.concatenate([g_hi, g_lo], axis=0).astype(bf16)
     gr = dims(g2, back_hi[...], 1, 0)
     gr = gr[0:16] + gr[16:32] + dims(g_hi.astype(bf16), back_lo[...], 1, 0)
     for g in (0, 1):
         send2[g] = gr[:, g * LANES : (g + 1) * LANES]
-    v0, v1 = gr[0:SUB, LANES:], gr[SUB:, LANES:]
-    quarter = lane8 // (2 * levp)
-    v32, v96, w32, w96 = (pltpu.roll(v, r, 1) for v in (v0, v1) for r in (2 * levp, 6 * levp))
-
-    def late(a, b):
-        return jnp.where(row8 < 3, pltpu.roll(a, 3, 0), pltpu.roll(b, 3, 0))
-
-    def pack_for(up_there):
-        near = jnp.where(up_there, v32, v96)
-        rest_cols = late(jnp.where(up_there, v96, v32), jnp.where(up_there, w96, w32))
-        q = jnp.where(up_there, quarter - 1, quarter)
-        return jnp.where(q == 2, near, jnp.where(q == 0, rest_cols, 0.0))
-
-    if xs == 1:
-        sendx[0] = pack_for(has_up)
-    else:
-        for side in (0, 1):
-            sendx[side] = pack_for(side == 0)
-
     def slot2(src):
         return recv2.at[src, :, pl.ds(0, frame), :]
 
@@ -656,6 +634,28 @@
             device_id={"mem": partner},
         )
 
+    for i, group in enumerate(classes):
+        for step in group:
+            copy2(2 * to_chip(step) + core, rs2.at[len(classes) - 1 - i]).start()
+    v0, v1 = gr[0:SUB, LANES:], gr[SUB:, LANES:]
+    quarter = lane8 // (2 * levp)
+    v32, v96, w32, w96 = (pltpu.roll(v, r, 1) for v in (v0, v1) for r in (2 * levp, 6 * levp))
+
+    def late(a, b):
+        return jnp.where(row8 < 3, pltpu.roll(a, 3, 0), pltpu.roll(b, 3, 0))
+
+    def pack_for(up_there):
+        near = jnp.where(up_there, v32, v96)
+        rest_cols = late(jnp.where(up_there, v96, v32), jnp.where(up_there, w96, w32))
+        q = jnp.where(up_there, quarter - 1, quarter)
+        return jnp.where(q == 2, near, jnp.where(q == 0, rest_cols, 0.0))
+
+    if xs == 1:
+        sendx[0] = pack_for(has_up)
+    else:
+        for side in (0, 1):
+            sendx[side] = pack_for(side == 0)
+
     for side in (0, 1):
 
         @pl.when(has[side])
@@ -663,9 +663,6 @@
             for step in far_first:
                 copyx(side, 2 * to_chip(step) + core).start()
 
-    for i, group in enumerate(classes):
-        for step in group:
-            copy2(2 * to_chip(step) + core, rs2.at[len(classes) - 1 - i]).start()
     copy2(partner, rs2f).start()
     for g in (0, 1):
         recv2[me, g] = send2[g]
@@ -698,6 +695,7 @@
         pltpu.make_async_copy(got, got, sem).wait()
 
     ensr[...] = pltpu.roll(whole(ensf), 1, 1) * scale
+    ebuf[...] = jnp.zeros(ebuf.shape, f32)
     edge_ens = [pltpu.roll(row(ensf, k), 1, 1) * scale for k in (0, rows - 1)]
     halo_ens = [pltpu.roll(edge_recv[side, 0:lev, :], 1, 1) * scale for side in (0, 1)]
 
@@ -720,8 +718,9 @@
 
     over = iota((SUB, LANES), 0) < frame - block
 
-    def across(ref):
-        cols = [ref[t * LANES : (t + 1) * LANES, :].T for t in range(tiles)]
+    def across(parts):
+        per_tile = LANES // SUB
+        cols = [jnp.concatenate(parts[t * per_tile : (t + 1) * per_tile], axis=0).T for t in range(tiles)]
         return cols[0] if tiles == 1 else jnp.concatenate(cols, axis=1)
 
     ours = (quarter < 2) | (set_of == 0) | (set_of == 3)
@@ -735,6 +734,7 @@
     def gather(g):
         sides = range(xs) if g else ()
         prev = [edges_at(i, n - 1)[1] for i in sides]
+        parts = []
         for d in range(n):
             tile = recv2[d, g, 0:SUB, :] + jnp.where(over, recv2[(d - 1) % n, g, SUB : 2 * SUB, :], 0.0)
             if g:
@@ -747,8 +747,8 @@
                     theirs = v if theirs is None else theirs + v
                     prev[i] = tail
                 tile = jnp.where(ours, tile, 0.0) + jnp.where(set_lanes, theirs, 0.0)
-            merged[g, d * SUB : (d + 1) * SUB, :] = tile
-        return across(merged.at[g])
+            parts.append(tile)
+        return across(parts)
 
     c0 = gather(0)
     for side in (0, 1):
@@ -760,23 +760,19 @@
 
     c1 = gather(1)
     e0 = main - LANES
-    coarse = jnp.concatenate([c0, c1[0:e0]], axis=0)
-    wm = ensr[...] * coarse
-    w_up = jnp.where(kk == 0, 0.0, pltpu.roll(wm, 1, 0))
-    w_dn = jnp.where(kk == rows - 1, 0.0, pltpu.roll(wm, main - 1, 0))
-    zz = smooth_back(0.25 * (w_up + w_dn) + 0.5 * wm)
-    for t in range(tiles):
-        grad_ref[t] = zz[:, t * LANES : (t + 1) * LANES]
     for side, k, k_in in ((0, 0, 1), (1, rows - 1, rows - 2)):
         halo_at, extra_at = (e0, e0 + levp) if side == 0 else (e0 + 3 * levp, e0 + 2 * levp)
         we = edge_ens[side] * c1[extra_at : extra_at + lev]
         wh = halo_ens[side] * c1[halo_at : halo_at + lev]
-        z_edge = smooth_back(0.5 * we + 0.25 * wh)
-        z_in = smooth_back(0.25 * we)
-        for t in range(tiles):
-            cut = slice(t * LANES, (t + 1) * LANES)
-            grad_ref.at[t][pl.ds(k, lev, stride=rows), :] += z_edge[:, cut]
-            grad_ref.at[t][pl.ds(k_in, lev, stride=rows), :] += z_in[:, cut]
+        for at, v in ((k, 0.5 * we + 0.25 * wh), (k_in, 0.25 * we)):
+            for t in range(tiles):
+                ebuf.at[t][pl.ds(at, lev, stride=rows), :] = v[:, t * LANES : (t + 1) * LANES]
+    wm = ensr[...] * jnp.concatenate([c0, c1[0:e0]], axis=0)
+    w_up = jnp.where(kk == 0, 0.0, pltpu.roll(wm, 1, 0))
+    w_dn = jnp.where(kk == rows - 1, 0.0, pltpu.roll(wm, main - 1, 0))
+    zz = smooth_back(0.25 * (w_up + w_dn) + 0.5 * wm + whole(ebuf))
+    for t in range(tiles):
+        grad_ref[t] = zz[:, t * LANES : (t + 1) * LANES]
 
     for side in (0, 1):
 
@@ -876,14 +872,12 @@
             pltpu.VMEM((4 * SUB, wide), f32),
             pltpu.VMEM((2, SUB, LANES), f32),
             pltpu.VMEM((2, SUB, LANES), f32),
-            pltpu.VMEM((fr, wide), f32),
-            pltpu.VMEM((fr, wide), f32),
             pltpu.VMEM((4 * SUB, wide), f32),
             pltpu.VMEM((2, fr, LANES), f32),
             pltpu.VMEM((n, 2, fr, LANES), f32),
             pltpu.VMEM((xs, SUB, LANES), f32),
             pltpu.VMEM((xs, 2, n // 2, SUB, LANES), f32),
-            pltpu.VMEM((2, lon, LANES), f32),
+            pltpu.VMEM((tiles, main, LANES), f32),
             pltpu.VMEM((main, lon), f32),
             dma((8,)),
             dma((xs,)),

time: 20.4 us -> 20.5 us (level)
  no operation moved by 1% of the time
where the time goes in v7:
time: 20.5 us; the launch traced here: 20.2 us
  Pallas kernels  19.5 us (95%)
  between operations  0.64 us (3%)
    pallas_call x1, Pallas kernels, shards(): pl.pallas_call(functools.partial(kernel, cfg), out_shape=(jax.ShapeDtypeS...  18.8 us
    pallas_call x1, Pallas kernels, shards(): pl.pallas_call(writer, out_shape=(jax.ShapeDtypeStruct(background.shape,...  0.67 us

profile of v7, /device:TPU:0, one launch (start us, length us, event | category | flops | bytes accessed | tf_op | source)
XLA Modules:
  0.0 20.2 jit_solution(53244120498771924)
XLA Ops:
  0.6 18.8 %shard_map.95 = (f32[12,1,1152]{2,1,0:T(1,128)S(1)}, f32[1,192,128]{2,1,0:T(8,128)S(1)}) custom-call(bf16[1,192,128]{2,1,0:T(8,128)(2,1)} %bitcast.6, f32[1,192,128]{2,1,0:T(8,128)} %bitcast.5, s32[1,48]{1,0:T(1,128)} %bitcast.7, f32[1,48]{1,0:T(1,128)} %bitcast.8, f32[12,1,1152]{2,1,0:T(1,128)} %bg_hbm.1, s32[1,256]{1,0:T(1,128)} %cell_hbm.1, ...), custom_call_target="tpu_custom_call" | custom-call | tf_op jit(solution)/shard_map/pallas_call | solution.py:831
  19.5 0.7 %shard_map.96 = (f32[12,1,1152]{2,1,0:T(1,128)}, f32[1,192,128]{2,1,0:T(8,128)}) custom-call(f32[12,1,1152]{2,1,0:T(1,128)S(1)} %get-tuple-element.6.adv_ref, f32[1,192,128]{2,1,0:T(8,128)S(1)} %get-tuple-element.7.grad_ref), custom_call_target="tpu_custom_call" | custom-call | tf_op jit(solution)/shard_map/pallas_call | solution.py:912

commit v8 on v7

--- a/solution.py
+++ b/solution.py
@@ -634,9 +634,12 @@
             device_id={"mem": partner},
         )
 
-    for i, group in enumerate(classes):
-        for step in group:
+    def send_class(i):
+        for step in classes[i]:
             copy2(2 * to_chip(step) + core, rs2.at[len(classes) - 1 - i]).start()
+
+    for i in range(len(classes) - 1):
+        send_class(i)
     v0, v1 = gr[0:SUB, LANES:], gr[SUB:, LANES:]
     quarter = lane8 // (2 * levp)
     v32, v96, w32, w96 = (pltpu.roll(v, r, 1) for v in (v0, v1) for r in (2 * levp, 6 * levp))
@@ -663,6 +666,7 @@
             for step in far_first:
                 copyx(side, 2 * to_chip(step) + core).start()
 
+    send_class(len(classes) - 1)
     copy2(partner, rs2f).start()
     for g in (0, 1):
         recv2[me, g] = send2[g]
@@ -760,19 +764,22 @@
 
     c1 = gather(1)
     e0 = main - LANES
+    wm = ensr[...] * jnp.concatenate([c0, c1[0:e0]], axis=0)
+    w_up = jnp.where(kk == 0, 0.0, pltpu.roll(wm, 1, 0))
+    w_dn = jnp.where(kk == rows - 1, 0.0, pltpu.roll(wm, main - 1, 0))
+    zz = smooth_back(0.25 * (w_up + w_dn) + 0.5 * wm)
+    for t in range(tiles):
+        grad_ref[t] = zz[:, t * LANES : (t + 1) * LANES]
     for side, k, k_in in ((0, 0, 1), (1, rows - 1, rows - 2)):
         halo_at, extra_at = (e0, e0 + levp) if side == 0 else (e0 + 3 * levp, e0 + 2 * levp)
         we = edge_ens[side] * c1[extra_at : extra_at + lev]
         wh = halo_ens[side] * c1[halo_at : halo_at + lev]
-        for at, v in ((k, 0.5 * we + 0.25 * wh), (k_in, 0.25 * we)):
-            for t in range(tiles):
-                ebuf.at[t][pl.ds(at, lev, stride=rows), :] = v[:, t * LANES : (t + 1) * LANES]
-    wm = ensr[...] * jnp.concatenate([c0, c1[0:e0]], axis=0)
-    w_up = jnp.where(kk == 0, 0.0, pltpu.roll(wm, 1, 0))
-    w_dn = jnp.where(kk == rows - 1, 0.0, pltpu.roll(wm, main - 1, 0))
-    zz = smooth_back(0.25 * (w_up + w_dn) + 0.5 * wm + whole(ebuf))
-    for t in range(tiles):
-        grad_ref[t] = zz[:, t * LANES : (t + 1) * LANES]
+        z_edge = smooth_back(0.5 * we + 0.25 * wh)
+        z_in = smooth_back(0.25 * we)
+        for t in range(tiles):
+            cut = slice(t * LANES, (t + 1) * LANES)
+            grad_ref.at[t][pl.ds(k, lev, stride=rows), :] += z_edge[:, cut]
+            grad_ref.at[t][pl.ds(k_in, lev, stride=rows), :] += z_in[:, cut]
 
     for side in (0, 1):
 

time: 20.5 us -> 20.2 us (0.985)
    pallas_call x1, Pallas kernels: 18.8 us -> 18.6 us  [shards(): pl.pallas_call(functools.partial(kernel, cfg), out_shape=(jax.ShapeDtypeS...]
where the time goes in v8:
time: 20.2 us; the launch traced here: 19.9 us
  Pallas kernels  19.3 us (96%)
  between operations  0.64 us (3%)
    pallas_call x1, Pallas kernels, shards(): pl.pallas_call(functools.partial(kernel, cfg), out_shape=(jax.ShapeDtypeS...  18.6 us
    pallas_call x1, Pallas kernels, shards(): pl.pallas_call(writer, out_shape=(jax.ShapeDtypeStruct(background.shape,...  0.67 us

profile of v8, /device:TPU:0, one launch (start us, length us, event | category | flops | bytes accessed | tf_op | source)
XLA Modules:
  0.0 19.9 jit_solution(3627865808930857396)
XLA Ops:
  0.6 18.6 %shard_map.95 = (f32[12,1,1152]{2,1,0:T(1,128)S(1)}, f32[1,192,128]{2,1,0:T(8,128)S(1)}) custom-call(bf16[1,192,128]{2,1,0:T(8,128)(2,1)} %bitcast.6, f32[1,192,128]{2,1,0:T(8,128)} %bitcast.5, s32[1,48]{1,0:T(1,128)} %bitcast.7, f32[1,48]{1,0:T(1,128)} %bitcast.8, f32[12,1,1152]{2,1,0:T(1,128)} %bg_hbm.1, s32[1,256]{1,0:T(1,128)} %cell_hbm.1, ...), custom_call_target="tpu_custom_call" | custom-call | tf_op jit(solution)/shard_map/pallas_call | solution.py:838
  19.3 0.7 %shard_map.96 = (f32[12,1,1152]{2,1,0:T(1,128)}, f32[1,192,128]{2,1,0:T(8,128)}) custom-call(f32[12,1,1152]{2,1,0:T(1,128)S(1)} %get-tuple-element.6.adv_ref, f32[1,192,128]{2,1,0:T(8,128)S(1)} %get-tuple-element.7.grad_ref), custom_call_target="tpu_custom_call" | custom-call | tf_op jit(solution)/shard_map/pallas_call | solution.py:919

commit v9 on v8

--- a/solution.py
+++ b/solution.py
@@ -324,7 +324,7 @@
         pl.semaphore_wait(barrier, n - 1 + n * (has_up.astype(jnp.int32) + has_down.astype(jnp.int32)))
 
     pre_copy = pltpu.make_async_remote_copy(
-        src_ref=frames.at[:, 1 - core],
+        src_ref=frames.at[:, core],
         dst_ref=pre_recv,
         send_sem=in_sem.at[0],
         recv_sem=pre_rs,
@@ -469,7 +469,7 @@
 
     pre_copy.wait_recv()
     for j in range(n // 2):
-        psum[j] = frames[j, core] + pre_recv[j]
+        psum[j] = frames[j, 1 - core] + pre_recv[j]
 
     used = frame + packed_rows
 
@@ -479,12 +479,11 @@
             dst_ref=recv1.at[chip, pl.ds(0, used), :],
             send_sem=in_sem.at[4],
             recv_sem=rs1,
-            device_id={"mem": 2 * dst + core},
-        )
-
-    for step in far_first[:-1]:
+            device_id={"mem": 2 * dst + 1 - core},
+        )
+
+    for step in far_first:
         copy1(to_chip(step)).start()
-    recv1[chip] = psum[chip]
 
     nobs = cell.shape[1]
     crow = cell[...] // fine_cols
@@ -555,7 +554,7 @@
     edge_a = pltpu.roll(edge_sum, half, 1)
     edge_b = pltpu.roll(edge_sum, 5, 0)
 
-    all_of(recv1, n // 2 - 1, used, rs1)
+    all_of(recv1, n // 2, used, rs1)
     total = recv1[0]
     for s in range(1, n // 2):
         total = total + recv1[s]
@@ -625,7 +624,7 @@
         )
 
     def forwardx(i):
-        got = recvx.at[i, core, :, pl.ds(0, packed_rows), :]
+        got = recvx.at[i, 1 - core, :, pl.ds(0, packed_rows), :]
         return pltpu.make_async_remote_copy(
             src_ref=got,
             dst_ref=got,
@@ -636,7 +635,7 @@
 
     def send_class(i):
         for step in classes[i]:
-            copy2(2 * to_chip(step) + core, rs2.at[len(classes) - 1 - i]).start()
+            copy2(2 * to_chip(step) + 1 - core, rs2.at[len(classes) - 1 - i]).start()
 
     for i in range(len(classes) - 1):
         send_class(i)
@@ -664,7 +663,7 @@
         @pl.when(has[side])
         def _():
             for step in far_first:
-                copyx(side, 2 * to_chip(step) + core).start()
+                copyx(side, 2 * to_chip(step) + 1 - core).start()
 
     send_class(len(classes) - 1)
     copy2(partner, rs2f).start()
@@ -683,7 +682,7 @@
     def sent_edges():
         pre_copy.wait_send()
         all_of(rece, n - 1, packed_rows, in_sem.at[1])
-        all_of(recv1, n // 2 - 1, used, in_sem.at[4])
+        all_of(recv1, n // 2, used, in_sem.at[4])
         pltpu.make_async_copy(fe_recv, fe_recv, in_sem.at[5]).wait()
         for side in (0, 1):
 
@@ -709,13 +708,14 @@
     for i, group in enumerate(reversed(classes)):
         all_2(len(group), rs2.at[i])
         for step in group:
-            forward2(2 * from_chip(step) + core).start()
+            forward2(2 * from_chip(step) + 1 - core).start()
     for side in (0, 1):
 
         @pl.when(has[side])
         def _():
             i = 0 if xs == 1 else side
-            pltpu.make_async_copy(recvx.at[i, core, :, pl.ds(0, packed_rows), :], recvx.at[i, core, :, pl.ds(0, packed_rows), :], rsx.at[i]).wait()
+            got = recvx.at[i, 1 - core, :, pl.ds(0, packed_rows), :]
+            pltpu.make_async_copy(got, got, rsx.at[i]).wait()
             forwardx(i).start()
 
     all_2(n // 2, rs2f)

time: 20.2 us -> 20 us (0.990)
  no operation moved by 1% of the time
where the time goes in v9:
time: 20 us; the launch traced here: 19.8 us
  Pallas kernels  19.2 us (96%)
  between operations  0.64 us (3%)
    pallas_call x1, Pallas kernels, shards(): pl.pallas_call(functools.partial(kernel, cfg), out_shape=(jax.ShapeDtypeS...  18.5 us
    pallas_call x1, Pallas kernels, shards(): pl.pallas_call(writer, out_shape=(jax.ShapeDtypeStruct(background.shape,...  0.67 us

profile of v9, /device:TPU:0, one launch (start us, length us, event | category | flops | bytes accessed | tf_op | source)
XLA Modules:
  0.0 19.8 jit_solution(4853223603352966505)
XLA Ops:
  0.6 18.5 %shard_map.95 = (f32[12,1,1152]{2,1,0:T(1,128)S(1)}, f32[1,192,128]{2,1,0:T(8,128)S(1)}) custom-call(bf16[1,192,128]{2,1,0:T(8,128)(2,1)} %bitcast.6, f32[1,192,128]{2,1,0:T(8,128)} %bitcast.5, s32[1,48]{1,0:T(1,128)} %bitcast.7, f32[1,48]{1,0:T(1,128)} %bitcast.8, f32[12,1,1152]{2,1,0:T(1,128)} %bg_hbm.1, s32[1,256]{1,0:T(1,128)} %cell_hbm.1, ...), custom_call_target="tpu_custom_call" | custom-call | tf_op jit(solution)/shard_map/pallas_call | solution.py:838
  19.2 0.7 %shard_map.96 = (f32[12,1,1152]{2,1,0:T(1,128)}, f32[1,192,128]{2,1,0:T(8,128)}) custom-call(f32[12,1,1152]{2,1,0:T(1,128)S(1)} %get-tuple-element.6.adv_ref, f32[1,192,128]{2,1,0:T(8,128)S(1)} %get-tuple-element.7.grad_ref), custom_call_target="tpu_custom_call" | custom-call | tf_op jit(solution)/shard_map/pallas_call | solution.py:919

commit v10 on v9

--- a/solution.py
+++ b/solution.py
@@ -637,8 +637,6 @@
         for step in classes[i]:
             copy2(2 * to_chip(step) + 1 - core, rs2.at[len(classes) - 1 - i]).start()
 
-    for i in range(len(classes) - 1):
-        send_class(i)
     v0, v1 = gr[0:SUB, LANES:], gr[SUB:, LANES:]
     quarter = lane8 // (2 * levp)
     v32, v96, w32, w96 = (pltpu.roll(v, r, 1) for v in (v0, v1) for r in (2 * levp, 6 * levp))
@@ -665,7 +663,8 @@
             for step in far_first:
                 copyx(side, 2 * to_chip(step) + 1 - core).start()
 
-    send_class(len(classes) - 1)
+    for i in range(len(classes)):
+        send_class(i)
     copy2(partner, rs2f).start()
     for g in (0, 1):
         recv2[me, g] = send2[g]

time: 20 us -> 20.1 us (level)
  no operation moved by 1% of the time
where the time goes in v10:
time: 20.1 us; the launch traced here: 20 us
  Pallas kernels  19.3 us (96%)
  between operations  0.64 us (3%)
    pallas_call x1, Pallas kernels, shards(): pl.pallas_call(functools.partial(kernel, cfg), out_shape=(jax.ShapeDtypeS...  18.7 us
    pallas_call x1, Pallas kernels, shards(): pl.pallas_call(writer, out_shape=(jax.ShapeDtypeStruct(background.shape,...  0.67 us

profile of v10, /device:TPU:0, one launch (start us, length us, event | category | flops | bytes accessed | tf_op | source)
XLA Modules:
  0.0 20.0 jit_solution(12594557129765392454)
XLA Ops:
  0.6 18.7 %shard_map.95 = (f32[12,1,1152]{2,1,0:T(1,128)S(1)}, f32[1,192,128]{2,1,0:T(8,128)S(1)}) custom-call(bf16[1,192,128]{2,1,0:T(8,128)(2,1)} %bitcast.6, f32[1,192,128]{2,1,0:T(8,128)} %bitcast.5, s32[1,48]{1,0:T(1,128)} %bitcast.7, f32[1,48]{1,0:T(1,128)} %bitcast.8, f32[12,1,1152]{2,1,0:T(1,128)} %bg_hbm.1, s32[1,256]{1,0:T(1,128)} %cell_hbm.1, ...), custom_call_target="tpu_custom_call" | custom-call | tf_op jit(solution)/shard_map/pallas_call | solution.py:837
  19.3 0.7 %shard_map.96 = (f32[12,1,1152]{2,1,0:T(1,128)}, f32[1,192,128]{2,1,0:T(8,128)}) custom-call(f32[12,1,1152]{2,1,0:T(1,128)S(1)} %get-tuple-element.6.adv_ref, f32[1,192,128]{2,1,0:T(8,128)S(1)} %get-tuple-element.7.grad_ref), custom_call_target="tpu_custom_call" | custom-call | tf_op jit(solution)/shard_map/pallas_call | solution.py:918

commit v11 on v10

--- a/solution.py
+++ b/solution.py
@@ -25,6 +25,12 @@
 def split2f(x):
     hi = x.astype(bf16).astype(f32)
     return hi, x - hi
+
+
+def split3f(x):
+    hi, rest = split2f(x)
+    mid, lo = split2f(rest)
+    return hi, mid, lo
 
 
 def dims(a, b, ca, cb):
@@ -304,17 +310,18 @@
     row32 = iota((4 * SUB, gcells), 0)
     col_of = jnp.where(row32 < ratio * SUB, (row32 % SUB) * ratio + row32 // SUB, -1)
     pick = (iota((4 * SUB, gcells), 1) % fine_cols == col_of).astype(f32).astype(bf16)
-    pick2 = jnp.concatenate([pick, pick], axis=1)
+    pick3 = jnp.concatenate([pick] * 3, axis=1)
     in_row = iota((RG, gcells), 1) // fine_cols == iota((RG, gcells), 0)
-    zbuf[main:, :] = jnp.zeros((gl - main, 2 * gcells), bf16)
+    zbuf[main:, :] = jnp.zeros((gl - main, 3 * gcells), bf16)
     back = bg[:, 0, :]
     for g in range(ng):
-        hi, lo = split2f(back[:, g * gcells : (g + 1) * gcells])
+        terms = split3f(back[:, g * gcells : (g + 1) * gcells])
         for l in range(lev):
             at = slice(l * RG, (l + 1) * RG)
-            zbuf[at, 0:gcells] = jnp.where(in_row, jnp.broadcast_to(hi[l : l + 1], (RG, gcells)), 0.0).astype(bf16)
-            zbuf[at, gcells : 2 * gcells] = jnp.where(in_row, jnp.broadcast_to(lo[l : l + 1], (RG, gcells)), 0.0).astype(bf16)
-        fine_bg[:, g * gl : (g + 1) * gl] = dims(pick2, zbuf[...], 1, 1)
+            for i, v in enumerate(terms):
+                spread = jnp.where(in_row, jnp.broadcast_to(v[l : l + 1], (RG, gcells)), 0.0)
+                zbuf[at, i * gcells : (i + 1) * gcells] = spread.astype(bf16)
+        fine_bg[:, g * gl : (g + 1) * gl] = dims(pick3, zbuf[...], 1, 1)
     for c in loads[3:]:
         c.wait()
 
@@ -491,24 +498,23 @@
     r32 = iota((4 * SUB, nobs), 0)
     col_o = jnp.where(r32 < ratio * SUB, (r32 % SUB) * ratio + r32 // SUB, -1)
     hot = (col_o == ccol).astype(f32).astype(bf16)
-    hot2 = jnp.concatenate([hot, hot], axis=1)
+    hot3 = jnp.concatenate([hot] * 3, axis=1)
     pr = prec[...]
-    p_hi, p_lo = split2f(pr)
-    v_hi, v_lo = split2f(val[:, 0, :] * pr)
-    rbuf[main:, :] = jnp.zeros((gl - main, 2 * nobs), bf16)
+    p_terms = split3f(pr)
+    v_terms = split3f(val[:, 0, :] * pr)
+    rbuf[main:, :] = jnp.zeros((gl - main, 3 * nobs), bf16)
     for g in range(ng):
         at_row = iota((RG, nobs), 0) + g * RG == crow
-        for l in range(lev):
-            at = slice(l * RG, (l + 1) * RG)
-            rbuf[at, 0:nobs] = jnp.where(at_row, jnp.broadcast_to(v_hi[l : l + 1], (RG, nobs)), 0.0).astype(bf16)
-            rbuf[at, nobs : 2 * nobs] = jnp.where(at_row, jnp.broadcast_to(v_lo[l : l + 1], (RG, nobs)), 0.0).astype(bf16)
-        obs_b[:, g * gl : (g + 1) * gl] = dims(hot2, rbuf[...], 1, 1)
-        ph = jnp.where(at_row, jnp.broadcast_to(p_hi, (RG, nobs)), 0.0).astype(bf16)
-        plo = jnp.where(at_row, jnp.broadcast_to(p_lo, (RG, nobs)), 0.0).astype(bf16)
-        for j in range(LANES // RG):
-            abuf[j * RG : (j + 1) * RG, 0:nobs] = ph
-            abuf[j * RG : (j + 1) * RG, nobs : 2 * nobs] = plo
-        oa = dims(hot2, abuf[...], 1, 1)
+        for i in range(3):
+            cut = slice(i * nobs, (i + 1) * nobs)
+            for l in range(lev):
+                v = jnp.broadcast_to(v_terms[i][l : l + 1], (RG, nobs))
+                rbuf[l * RG : (l + 1) * RG, cut] = jnp.where(at_row, v, 0.0).astype(bf16)
+            p = jnp.where(at_row, jnp.broadcast_to(p_terms[i], (RG, nobs)), 0.0).astype(bf16)
+            for j in range(LANES // RG):
+                abuf[j * RG : (j + 1) * RG, cut] = p
+        obs_b[:, g * gl : (g + 1) * gl] = dims(hot3, rbuf[...], 1, 1)
+        oa = dims(hot3, abuf[...], 1, 1)
         for j in range(gl // LANES):
             obs_a[:, g * gl + j * LANES : g * gl + (j + 1) * LANES] = oa
 
@@ -870,9 +876,9 @@
             pltpu.VMEM((kaps, wide), bf16),
             pltpu.VMEM((wide, kaps), bf16),
             pltpu.VMEM((wide, kaps), bf16),
-            pltpu.VMEM((gl, 2 * gcells), bf16),
-            pltpu.VMEM((gl, 2 * nobs), bf16),
-            pltpu.VMEM((LANES, 2 * nobs), bf16),
+            pltpu.VMEM((gl, 3 * gcells), bf16),
+            pltpu.VMEM((gl, 3 * nobs), bf16),
+            pltpu.VMEM((LANES, 3 * nobs), bf16),
             pltpu.VMEM((4 * SUB, wide), f32),
             pltpu.VMEM((4 * SUB, wide), f32),
             pltpu.VMEM((4 * SUB, wide), f32),

time: 20.1 us -> 20.1 us (level)
  no operation moved by 1% of the time
where the time goes in v11:
time: 20.1 us; the launch traced here: 20 us
  Pallas kernels  19.3 us (96%)
  between operations  0.64 us (3%)
    pallas_call x1, Pallas kernels, shards(): pl.pallas_call(functools.partial(kernel, cfg), out_shape=(jax.ShapeDtypeS...  18.7 us
    pallas_call x1, Pallas kernels, shards(): pl.pallas_call(writer, out_shape=(jax.ShapeDtypeStruct(background.shape,...  0.67 us

profile of v11, /device:TPU:0, one launch (start us, length us, event | category | flops | bytes accessed | tf_op | source)
XLA Modules:
  0.0 20.0 jit_solution(16493405194943324464)
XLA Ops:
  0.6 18.7 %shard_map.95 = (f32[12,1,1152]{2,1,0:T(1,128)S(1)}, f32[1,192,128]{2,1,0:T(8,128)S(1)}) custom-call(bf16[1,192,128]{2,1,0:T(8,128)(2,1)} %bitcast.6, f32[1,192,128]{2,1,0:T(8,128)} %bitcast.5, s32[1,48]{1,0:T(1,128)} %bitcast.7, f32[1,48]{1,0:T(1,128)} %bitcast.8, f32[12,1,1152]{2,1,0:T(1,128)} %bg_hbm.1, s32[1,256]{1,0:T(1,128)} %cell_hbm.1, ...), custom_call_target="tpu_custom_call" | custom-call | tf_op jit(solution)/shard_map/pallas_call | solution.py:843
  19.3 0.7 %shard_map.96 = (f32[12,1,1152]{2,1,0:T(1,128)}, f32[1,192,128]{2,1,0:T(8,128)}) custom-call(f32[12,1,1152]{2,1,0:T(1,128)S(1)} %get-tuple-element.6.adv_ref, f32[1,192,128]{2,1,0:T(8,128)S(1)} %get-tuple-element.7.grad_ref), custom_call_target="tpu_custom_call" | custom-call | tf_op jit(solution)/shard_map/pallas_call | solution.py:924
